TPU v7x, 16 devices: a whole 2x2x2 slice. The times are simulated.
16 devices in a mesh: dp: 1, ep: 16 (over x, y, z, core).
Axes of the slice: x: 2, y: 2, z: 2, core: 2. Of those that a mesh axis runs over, the one named last changes fastest.
Arguments:
- x: bfloat16 [1, 16, 256, 2048], P('dp', 'ep')
- expert: int32 [1, 16, 256, 6], P('dp', 'ep')
- slot: int32 [1, 16, 256, 6], P('dp', 'ep')
- gate: float32 [1, 16, 256, 6], P('dp', 'ep')
- w_gate: bfloat16 [64, 2048, 1408], P('ep')
- w_up: bfloat16 [64, 2048, 1408], P('ep')
- w_down: bfloat16 [64, 1408, 2048], P('ep')
- s_gate: bfloat16 [2048, 2816], replicated
- s_up: bfloat16 [2048, 2816], replicated
- s_down: bfloat16 [2816, 2048], replicated
Outputs:
- y: bfloat16 [1, 16, 256, 2048], P('dp', 'ep')
All inputs are finite; a program needn't handle non-finite values.
Results may differ from a plain program's by a relative error of at most 0.009.
Values are sent between devices in bfloat16 or wider.
A program may use at most 2 GiB of HBM per device.

v0:
```python
import jax
import jax.numpy as jnp
from jax import lax
from jax.sharding import NamedSharding, PartitionSpec as P


def einsum(form, a, b):
    return jnp.einsum(form, a.astype(jnp.float32), b.astype(jnp.float32))


def for_all(x, s_gate, s_up, s_down):
    h = jax.nn.silu(einsum("...d,df->...f", x, s_gate)) * einsum("...d,df->...f", x, s_up)
    return einsum("...f,fd->...d", h.astype(jnp.bfloat16), s_down)


def solution(mesh):
    def placed(v, *spec):
        return lax.with_sharding_constraint(v, NamedSharding(mesh, P(*spec)))

    def step(x, expert, slot, gate, w_gate, w_up, w_down, s_gate, s_up, s_down):
        experts, (tokens, top) = w_gate.shape[0], expert.shape[2:]
        slots = 5 * tokens * top // (4 * experts)
        to_expert = jax.nn.one_hot(expert, experts, dtype=jnp.bfloat16)
        to_slot = jax.nn.one_hot(slot, slots, dtype=jnp.bfloat16)
        weighted = to_expert * gate[..., None].astype(jnp.bfloat16)
        dispatch = einsum("abtke,abtkc->abtec", to_expert, to_slot).astype(jnp.bfloat16)
        combine = einsum("abtke,abtkc->abtec", weighted, to_slot).astype(jnp.bfloat16)
        z = einsum("abtec,abtd->aebcd", dispatch, x).astype(jnp.bfloat16)
        z = placed(z, "dp", None, "ep", None, None)
        z = placed(z, "dp", "ep", None, None, None)
        h = jax.nn.silu(einsum("aebcd,edf->aebcf", z, w_gate))
        h = (h * einsum("aebcd,edf->aebcf", z, w_up)).astype(jnp.bfloat16)
        out = einsum("aebcf,efd->aebcd", h, w_down).astype(jnp.bfloat16)
        out = placed(out, "dp", "ep", None, None, None)
        out = placed(out, "dp", None, "ep", None, None)
        y = einsum("abtec,aebcd->abtd", combine, out)
        return (y + for_all(x, s_gate, s_up, s_down)).astype(jnp.bfloat16)

    return step
```

profile of v0, /device:TPU:0, one launch (start us, length us, event | category | flops | bytes accessed | tf_op | source)
XLA Modules:
  0.0 404.9 jit_solution(7062430270324043801)
XLA Ops:
  0.0 0.0 copy-start
  0.0 0.9 copy.21
  0.9 0.8 copy.23
  1.7 2.6 convolution_convert_fusion.1
  4.4 0.0 copy-done
  4.4 6.2 %convert_bitcast_fusion.1 = bf16[1,64,1,30,2048]{4,1,3,2,0:T(8,128)(2,1)} fusion(bf16[256,64,30]{1,2,0:T(8,128)(2,1)S(1)} %convolution_convert_fusion.1, bf16[1,1,256,2048]{3,2,1,0:T(8,128)(2,1)S(1)} %copy-done), kind=kOutput, calls=%fused_computation.16 | convolution fusion | flops 2017198080 | bytes 9895936 | tf_op jit(solution)/abtec,abtd->aebcd/dot_general | solution.py:8
  10.6 12.4 %reshape.67 = bf16[1,16,4,1,30,2048]{5,2,1,4,3,0:T(4,128)(2,1)} reshape(bf16[1,64,1,30,2048]{4,1,3,2,0:T(8,128)(2,1)} %convert_bitcast_fusion.1) | data formatting | bytes 15728640 | tf_op jit(solution)/sharding_constraint;jit(solution)/sharding_constraint | solution.py:18
  23.0 12.1 %copy.13 = bf16[1,16,4,1,30,2048]{5,2,4,3,0,1:T(4,128)(2,1)} copy(bf16[1,16,4,1,30,2048]{5,2,1,4,3,0:T(4,128)(2,1)} %reshape.67) | data formatting | bytes 15728640 | tf_op jit(solution)/sharding_constraint;jit(solution)/sharding_constraint | solution.py:18
  35.1 94.3 %all-to-all.4 = bf16[1,16,4,1,30,2048]{5,2,4,3,0,1:T(4,128)(2,1)} all-to-all(bf16[1,16,4,1,30,2048]{5,2,4,3,0,1:T(4,128)(2,1)} %copy.13), channel_id=1, replica_groups=mesh['dp'=1,'ep'=16] {'ep'}, dimensions={1} | all-to-all | bytes 15728640 | tf_op jit(solution)/sharding_constraint;jit(solution)/sharding_constraint | solution.py:18
  129.5 42.4 %fusion.2 = f32[4,16,30,1408]{3,2,1,0:T(8,128)} fusion(bf16[4,2048,1408]{2,1,0:T(8,128)(2,1)} %param.5, bf16[1,16,4,1,30,2048]{5,2,4,3,0,1:T(4,128)(2,1)} %all-to-all.4), kind=kOutput, calls=%fused_computation.2 | convolution fusion | flops 11072962560 | bytes 41746432 | tf_op jit(solution)/aebcd,edf->aebcf/dot_general | solution.py:8
  171.8 44.8 %fusion.6 = bf16[1,4,16,30,1408]{4,3,2,1,0:T(8,128)(2,1)} fusion(f32[4,16,30,1408]{3,2,1,0:T(8,128)} %fusion.2, bf16[4,2048,1408]{2,1,0:T(8,128)(2,1)} %param.4, bf16[1,16,4,1,30,2048]{5,2,4,3,0,1:T(4,128)(2,1)} %all-to-all.4), kind=kOutput, calls=%fused_computation.7 | convolution fusion | flops 11089182720 | bytes 47153152 | tf_op jit(solution)/aebcd,edf->aebcf/dot_general | solution.py:8
  216.6 21.5 %convert_bitcast_fusion = bf16[1,4,16,1,30,2048]{5,4,2,1,3,0:T(8,128)(2,1)} fusion(bf16[4,1408,2048]{2,1,0:T(8,128)(2,1)} %param.6, bf16[1,4,16,30,1408]{4,3,2,1,0:T(8,128)(2,1)} %fusion.6), kind=kOutput, calls=%fused_computation.15 | convolution fusion | flops 11076894720 | bytes 36339712 | tf_op jit(solution)/aebcf,efd->aebcd/dot_general | solution.py:8
  238.1 10.5 %copy.15 = bf16[1,4,16,1,30,2048]{5,1,4,3,0,2:T(4,128)(2,1)} copy(bf16[1,4,16,1,30,2048]{5,4,2,1,3,0:T(8,128)(2,1)} %convert_bitcast_fusion) | data formatting | bytes 15728640 | tf_op jit(solution)/sharding_constraint;jit(solution)/sharding_constraint | solution.py:18
  248.6 0.0 copy-start.1
  248.6 3.6 all-to-all-start.1
  252.2 0.0 copy-done.1
  252.2 0.1 copy.22
  252.4 3.0 convolution_convert_fusion
  255.4 9.0 %convolution_bitcast_fusion.1 = f32[1,256,2816]{2,1,0:T(8,128)} fusion(bf16[2048,2816]{1,0:T(8,128)(2,1)} %param.7, bf16[1,1,256,2048]{3,2,1,0:T(8,128)(2,1)S(1)} %copy-done), kind=kOutput, calls=%fused_computation.22 | convolution fusion | flops 2952790016 | bytes 15466496 | tf_op jit(solution)/...d,df->...f/dot_general | solution.py:8
  264.3 15.9 %fusion.39 = f32[256,2048]{1,0:T(8,128)} fusion(bf16[2816,2048]{1,0:T(8,128)(2,1)} %param.9, bf16[2048,2816]{1,0:T(8,128)(2,1)} %param.8, f32[1,256,2816]{2,1,0:T(8,128)} %convolution_bitcast_fusion.1, bf16[1,1,256,2048]{3,2,1,0:T(8,128)(2,1)S(1)} %copy-done), kind=kOutput, calls=%fused_computation.41 | convolution fusion | flops 5909905408 | bytes 29097984 | tf_op jit(solution)/...f,fd->...d/dot_general | solution.py:8
  280.2 92.8 %all-to-all-done.1 = bf16[1,4,16,1,30,2048]{5,1,4,3,0,2:T(4,128)(2,1)} async-done(((bf16[1,4,16,1,30,2048]{5,1,4,3,0,2:T(4,128)(2,1)}), bf16[1,4,16,1,30,2048]{5,1,4,3,0,2:T(4,128)(2,1)}, u32[]{:S(2)}, u32[]{:S(2)}) %all-to-all-start.1) | async-done | bytes 7864352 | tf_op jit(solution)/sharding_constraint;jit(solution)/sharding_constraint | solution.py:18
  373.0 12.1 %copy.16 = bf16[1,16,4,1,30,2048]{5,2,1,4,3,0:T(4,128)(2,1)} copy(bf16[1,16,4,1,30,2048]{5,2,4,3,0,1:T(4,128)(2,1)} %bitcast.34) | data formatting | bytes 15728640 | tf_op jit(solution)/sharding_constraint;jit(solution)/sharding_constraint | solution.py:18
  385.2 11.9 %reshape.92 = bf16[64,30,2048]{2,0,1:T(8,128)(2,1)} reshape(bf16[1,16,4,1,30,2048]{5,2,1,4,3,0:T(4,128)(2,1)} %copy.16) | data formatting | bytes 15728640
  397.0 7.7 %fusion.26 = bf16[1,1,256,2048]{3,2,1,0:T(8,128)(2,1)} fusion(f32[256,2048]{1,0:T(8,128)} %fusion.39, bf16[64,30,2048]{2,0,1:T(8,128)(2,1)} %reshape.92, bf16[256,64,30]{1,2,0:T(8,128)(2,1)S(1)} %convolution_convert_fusion), kind=kOutput, calls=%fused_computation.28 | convolution fusion | flops 2014314496 | bytes 11993088 | tf_op jit(solution)/abtec,aebcd->abtd/dot_general | solution.py:8
  (1 shorter events, 0.0 us)
Async XLA Ops:
  0.0 4.4 %copy-start = (bf16[1,1,256,2048]{3,2,1,0:T(8,128)(2,1)S(1)}, bf16[1,1,256,2048]{3,2,1,0:T(8,128)(2,1)}, u32[]{:S(2)}) copy-start(bf16[1,1,256,2048]{3,2,1,0:T(8,128)(2,1)} %param.3) | copy-start | bytes 3145732
  248.6 3.6 copy-start.1
  248.6 124.4 %all-to-all-start.1 = ((bf16[1,4,16,1,30,2048]{5,1,4,3,0,2:T(4,128)(2,1)}), bf16[1,4,16,1,30,2048]{5,1,4,3,0,2:T(4,128)(2,1)}, u32[]{:S(2)}, u32[]{:S(2)}) async-start(bf16[1,4,16,1,30,2048]{5,1,4,3,0,2:T(4,128)(2,1)} %copy.15), calls=%async_computation.1 | async-start | bytes 15728640 | tf_op jit(solution)/sharding_constraint;jit(solution)/sharding_constraint | solution.py:18
where the time goes:
time: 412 us; the launch traced here: 405 us
  matrix products  153 us (37%)
  blocking collectives  94.3 us (23%)
  waiting for transfers between devices  92.8 us (23%)
  local copies, waits for them, and re-layouts  61 us (15%)
    dot_general x9, matrix products, einsum(): return jnp.einsum(form, a.astype(jnp.float32), b.astype(jnp.float32))  153 us
    another operation x1, blocking collectives, placed(): return lax.with_sharding_constraint(v, NamedSharding(mesh, P(*spec)))  94.3 us
    another operation x1, waiting for transfers between devices, placed(): return lax.with_sharding_constraint(v, NamedSharding(mesh, P(*spec)))  92.8 us
    another operation x4, local copies, waits for them, and re-layouts, placed(): return lax.with_sharding_constraint(v, NamedSharding(mesh, P(*spec)))  47.2 us
    unnamed x5, local copies, waits for them, and re-layouts  11.9 us
  transfers between devices with their start and end apart: 1, of which 1 were waited for; matrix products, arithmetic and copies ran while one was open for 7% of the time, Pallas kernels for 0%

commit v1 on v0

v1 whole, which is shorter than its diff:
```python
import functools

import jax
import jax.numpy as jnp
from jax import lax
from jax.experimental import pallas as pl
from jax.experimental.pallas import tpu as pltpu
from jax.sharding import PartitionSpec as P

MESH = pl.DeviceIdType.MESH
F32, BF16 = jnp.float32, jnp.bfloat16

T, D, F, TOP = 256, 2048, 1408, 6
SLOTS, PAD, EXP = 30, 32, 4
ROWS = EXP * PAD
HALF = D // 2
PART = ((0, 88), (88, 88), (176, 80))
BIT = (4, 2, 1)
ORDER = tuple(tuple((p + i) % 3 for i in range(3)) for p in range(3))


def gather_messages(p):
    b0, b1, b2 = (BIT[d] for d in ORDER[p])
    table = ((0, 0), (0, 1), (b0, 1), (0, 2), (b0, 2), (b1, 2), (b0 | b1, 2))
    return tuple((s, i, s ^ BIT[ORDER[p][i]]) for s, i in table)


def scatter_messages(p):
    b0, b1, b2 = (BIT[d] for d in ORDER[p])
    return (
        (b0 | b1 | b2, 0, ()), (b0 | b1, 0, ()), (b0 | b2, 0, ()), (b0, 0, ()),
        (b1 | b2, 1, (0,)), (b1, 1, (1,)), (b2, 2, (2, 4)),
    )


GATHER = tuple(gather_messages(p) for p in range(3))
SCATTER = tuple(scatter_messages(p) for p in range(3))
N_TILES = tuple((n, min(256, F - n)) for n in range(0, F, 256))


def kernel(x, meta, wg, wu, wd, sg, su, sd, y, xg, *scratch):
    (gbuf, ubuf, dbuf, z, ob, dr, r0, r1, r2, s0, s1, s2, acc, xt, comb, h, fs, fr, mt,
     wsem, xsem, lsem, xs_s, xs_r, meta_s, meta_r, ag_s, ag_r, fw_s, fw_r, dr_s, dr_r, rs_s, rs_r, fin_s, fin_r) = scratch
    me = lax.axis_index("ep")
    c, q = me % 2, me // 2
    sib = me + 1 - 2 * c
    nbr = [me + (1 - 2 * ((me // (2 * b)) % 2)) * (2 * b) for b in BIT]
    mine = pl.ds(pl.multiple_of(c * HALF, HALF), HALF)
    theirs = pl.ds(pl.multiple_of((1 - c) * HALF, HALF), HALF)
    rbuf, sbuf = (r0, r1, r2), (s0, s1, s2)

    def remote(src, dst, send, recv, to):
        return pltpu.make_async_remote_copy(
            src_ref=src, dst_ref=dst, send_sem=send, recv_sem=recv, device_id={"ep": to}, device_id_type=MESH)

    def ag(k, p, m):
        s, i, land = GATHER[p][m]
        rows = pl.ds(*PART[p])
        return remote(xg.at[k, s, rows, mine], xg.at[k, land, rows, mine], ag_s.at[k, p, m], ag_r.at[k, p, m],
                      nbr[ORDER[p][i]])

    def fwd(k, p, m):
        rows = pl.ds(*PART[p])
        piece = xg.at[k, GATHER[p][m][2], rows, mine]
        return remote(piece, piece, fw_s.at[k, p, m], fw_r.at[k, p, m], sib)

    def fwd_in(k, p, m):
        rows = pl.ds(*PART[p])
        piece = xg.at[k, GATHER[p][m][2], rows, theirs]
        return remote(piece, piece, fw_s.at[k, p, m], fw_r.at[k, p, m], sib)

    def give(k, r):
        return remote(z.at[r // 2, :, pl.ds((r % 2) * HALF, HALF)], dr.at[k, r], dr_s.at[k, r], dr_r.at[k, r], sib)

    def rs(k, p, n):
        return remote(sbuf[p].at[n], rbuf[p].at[k, n], rs_s.at[k, p, n], rs_r.at[k, p, n],
                      nbr[ORDER[p][SCATTER[p][n][1]]])

    def meta_copy(i):
        return remote(meta, mt.at[i], meta_s.at[i], meta_r.at[i], xor(me, i, 4))

    def xor(v, mask, bits):
        out = v
        for b in range(bits):
            if mask >> b & 1:
                out = out + (1 - 2 * ((v // (1 << b)) % 2)) * (1 << b)
        return out

    own_send = remote(x, xg.at[c, 0], xs_s, xs_r, sib)
    own_recv = remote(x, xg.at[1 - c, 0], xs_s, xs_r, sib)
    x_in = pltpu.make_async_copy(x, xt.at[0], xsem.at[0])
    x_out = pltpu.make_async_copy(xt.at[0], xg.at[c, 0], lsem)
    final_send = remote(fs, fr, fin_s, fin_r, sib)

    def load_g(src):
        return pltpu.make_async_copy(src, gbuf, wsem.at[0])

    def load_u(src):
        return pltpu.make_async_copy(src, ubuf, wsem.at[1])

    def load_d(src):
        return pltpu.make_async_copy(src, dbuf, wsem.at[2])

    def shared_cols(ref, i):
        return ref.at[:, pl.ds(pl.multiple_of(i * F, 128), F)]

    def shared_rows(i):
        return sd.at[pl.ds(pl.multiple_of(i * F, 128), F), :]

    def start_gather(k):
        @pl.when(c != k)
        def _():
            own_recv.wait_recv()

        for m in (0, 1, 3):
            for p in range(3):
                ag(k, p, m).start()

    def arrive(k, m, sends):
        for p in range(3):
            ag(k, p, m).wait_recv()
            for n in sends:
                ag(k, p, n).start()
            fwd(k, p, m).start()

    def x_load(k, r, b):
        return pltpu.make_async_copy(xg.at[k, r], xt.at[b], xsem.at[b])

    def landed(k, r):
        for p in range(3):
            for m in range(7):
                if GATHER[p][m][2] == r:
                    fwd_in(k, p, m).wait_recv()

    def dispatch(k, r, b):
        x_load(k, r, b).wait()
        table = mt[2 * r + (k + c) % 2]
        row = (lax.broadcasted_iota(jnp.int32, (ROWS, T), 0) + me * ROWS).astype(F32)
        pick = jnp.zeros((ROWS, T), F32)
        weight = jnp.zeros((ROWS, T), F32)
        for j in range(TOP):
            hit = table[j:j + 1, :] == row
            pick = jnp.where(hit, 1.0, pick)
            weight = jnp.where(hit, table[8 + j:9 + j, :], weight)
        comb[k, r] = weight.T
        for n in range(0, D, 512):
            rows = jnp.dot(pick.astype(BF16), xt[b, :, n:n + 512], preferred_element_type=F32).astype(BF16)
            for e in range(EXP):
                z[e, r * PAD:(r + 1) * PAD, n:n + 512] = rows[e * PAD:(e + 1) * PAD]

    def hidden(load):
        for n, w in N_TILES:
            g = jnp.dot(load(), gbuf[:, n:n + w], preferred_element_type=F32)
            u = jnp.dot(load(), ubuf[:, n:n + w], preferred_element_type=F32)
            h[:, n:n + w] = (g * (1.0 / (1.0 + jnp.exp(-g))) * u).astype(BF16)

    def down(store):
        for n in range(0, D, 512):
            store(n, jnp.dot(h[...], dbuf[:, n:n + 512], preferred_element_type=F32))

    def give_all(k):
        for r in (7, 6, 5, 3, 4, 2, 1, 0):
            part = jnp.dot(comb[k, r].astype(BF16), ob[k, r, :, theirs], preferred_element_type=F32)
            z[r // 2, :, (r % 2) * HALF:(r % 2) * HALF + HALF] = part.astype(BF16)
            give(k, r).start()

    def term(k, p, r):
        first, rows = PART[p]
        low = first // 16 * 16
        part = jnp.dot(comb[k, r, first:first + rows, :].astype(BF16), ob[k, r, :, mine], preferred_element_type=F32)
        other = dr[k, r, low:first + rows, :].astype(F32)[first - low:]
        return part + other

    def send_sum(k, n):
        for p in range(3):
            r, _, joins = SCATTER[p][n]
            total = term(k, p, r)
            for j in joins:
                rs(k, p, j).wait_recv()
                total = total + rbuf[p][k, j].astype(F32)
            if k == 1:
                rs(0, p, n).wait_send()
            sbuf[p][n] = total.astype(BF16)
            rs(k, p, n).start()

    def start_scatter(k):
        give(k, 7).wait_recv()
        send_sum(k, 0)
        for r in (6, 5, 3):
            give(k, r).wait_recv()
        send_sum(k, 1)
        send_sum(k, 2)
        for r in (4, 2, 1):
            give(k, r).wait_recv()
        send_sum(k, 3)
        give(k, 0).wait_recv()

    def finish(k):
        for p in range(3):
            first, rows = PART[p]
            total = term(k, p, 0)
            for j in (3, 5, 6):
                rs(k, p, j).wait_recv()
                total = total + rbuf[p][k, j].astype(F32)

            @pl.when(c == k)
            def _():
                acc[first:first + rows, mine] += total

            @pl.when(c != k)
            def _():
                fs[p, :rows] = total.astype(BF16)

        @pl.when(c != k)
        def _():
            final_send.start()

    x_in.start()
    own_send.start()
    mt[0] = meta[...]
    load_g(shared_cols(sg, 0)).start()
    load_u(shared_cols(su, 0)).start()
    load_d(shared_rows(0)).start()
    for i in range(1, 16):
        meta_copy(i).start()
    x_in.wait()
    x_out.start()
    x_out.wait()
    start_gather(0)
    acc[...] = jnp.zeros_like(acc)

    @pl.loop(0, 2)
    def _(i):
        load_g(shared_cols(sg, i)).wait()
        load_u(shared_cols(su, i)).wait()
        hidden(lambda: xt[0])

        @pl.when(i == 0)
        def _():
            load_g(shared_cols(sg, 1)).start()
            load_u(shared_cols(su, 1)).start()

        @pl.when(i == 1)
        def _():
            load_g(wg.at[0]).start()
            load_u(wu.at[0]).start()
            arrive(0, 0, (2, 4))

        load_d(shared_rows(i)).wait()

        def store(n, v):
            acc[:, n:n + 512] += v

        down(store)

        @pl.when(i == 0)
        def _():
            load_d(shared_rows(1)).start()

        @pl.when(i == 1)
        def _():
            load_d(wd.at[0]).start()

    for i in range(1, 16):
        meta_copy(i).wait_recv()
    arrive(0, 1, (5,))
    x_load(0, 0, 0).start()
    arrive(0, 2, (6,))
    start_gather(1)
    arrive(0, 3, ())

    def dispatch_all(k, waits):
        order = (0, 4, 2, 1, 6, 5, 3, 7)
        for n, r in enumerate(order):
            if n + 1 < 8:
                nxt = order[n + 1]
                for m in waits.get(n + 1, ()):
                    arrive(k, m, ())
                landed(k, nxt)
                x_load(k, nxt, (n + 1) % 2).start()
            dispatch(k, r, n % 2)

    dispatch_all(0, {4: (4, 5), 7: (6,)})

    @pl.loop(0, 8)
    def _(i):
        k, e = i // 4, i % 4
        nxt = (i + 1) % 4
        load_g(wg.at[e]).wait()
        load_u(wu.at[e]).wait()
        hidden(lambda: z[e])

        @pl.when(i < 7)
        def _():
            load_g(wg.at[nxt]).start()
            load_u(wu.at[nxt]).start()

        @pl.when(i == 7)
        def _():
            send_sum(0, 6)

        load_d(wd.at[e]).wait()

        def store(n, v):
            for r in range(8):
                ob[k, r, pl.ds(pl.multiple_of(e * PAD, PAD), PAD), n:n + 512] = v[r * PAD:(r + 1) * PAD].astype(BF16)

        down(store)

        @pl.when(i < 7)
        def _():
            load_d(wd.at[nxt]).start()

        @pl.when(i == 0)
        def _():
            arrive(1, 0, (2, 4))

        @pl.when(i == 1)
        def _():
            arrive(1, 1, (5,))

        @pl.when(i == 2)
        def _():
            arrive(1, 2, (6,))
            arrive(1, 3, ())

        @pl.when(i == 3)
        def _():
            give_all(0)
            x_load(1, 0, 0).start()
            start_scatter(0)
            for r in range(8):
                give(0, r).wait_send()
            dispatch_all(1, {4: (4, 5), 7: (6,)})

        @pl.when(i == 4)
        def _():
            send_sum(0, 4)

        @pl.when(i == 5)
        def _():
            send_sum(0, 5)

    give_all(1)
    start_scatter(1)
    finish(0)
    send_sum(1, 4)
    send_sum(1, 5)
    send_sum(1, 6)
    finish(1)
    final_send.wait()
    for p in range(3):
        first, rows = PART[p]
        acc[first:first + rows, theirs] += fr[p, :rows].astype(F32)
    y[...] = acc[...].astype(BF16)

    own_send.wait_send()
    for i in range(1, 16):
        meta_copy(i).wait_send()
    for k in range(2):
        for p in range(3):
            for m in range(7):
                ag(k, p, m).wait_send()
                fwd(k, p, m).wait_send()
    for r in range(8):
        give(1, r).wait_send()
    for p in range(3):
        for n in range(7):
            rs(1, p, n).wait_send()


def solution(mesh):
    dma = pltpu.SemaphoreType.DMA

    def body(x, expert, slot, gate, wg, wu, wd, sg, su, sd):
        x = x.reshape(T, D)
        row = jnp.where(slot < SLOTS, expert * PAD + slot, -1).reshape(T, TOP).astype(F32)
        weight = gate.reshape(T, TOP).astype(BF16).astype(F32)
        blank = jnp.zeros((T, 8 - TOP), F32)
        meta = jnp.concatenate([row, blank, weight, blank], axis=1).T
        hbm, vmem = pl.BlockSpec(memory_space=pltpu.HBM), pl.BlockSpec(memory_space=pltpu.VMEM)
        y, _ = pl.pallas_call(
            kernel,
            name="moe",
            out_shape=(jax.ShapeDtypeStruct((T, D), BF16), jax.ShapeDtypeStruct((2, 8, T, D), BF16)),
            in_specs=[hbm, vmem, hbm, hbm, hbm, hbm, hbm, hbm],
            out_specs=(vmem, hbm),
            scratch_shapes=[
                pltpu.VMEM((D, F), BF16), pltpu.VMEM((D, F), BF16), pltpu.VMEM((F, D), BF16),
                pltpu.VMEM((EXP, T, D), BF16),
                pltpu.VMEM((2, 8, ROWS, D), BF16),
                pltpu.VMEM((2, 8, T, HALF), BF16),
                *[pltpu.VMEM((2, 7, n, HALF), BF16) for _, n in PART],
                *[pltpu.VMEM((7, n, HALF), BF16) for _, n in PART],
                pltpu.VMEM((T, D), F32),
                pltpu.VMEM((2, T, D), BF16),
                pltpu.VMEM((2, 8, T, ROWS), F32),
                pltpu.VMEM((T, F), BF16),
                pltpu.VMEM((3, 88, HALF), BF16), pltpu.VMEM((3, 88, HALF), BF16),
                pltpu.VMEM((16, 16, T), F32),
                dma((3,)), dma((2,)), dma, dma, dma, dma((16,)), dma((16,)),
                dma((2, 3, 7)), dma((2, 3, 7)), dma((2, 3, 7)), dma((2, 3, 7)),
                dma((2, 8)), dma((2, 8)), dma((2, 3, 7)), dma((2, 3, 7)), dma, dma,
            ],
            compiler_params=pltpu.CompilerParams(has_side_effects=True, vmem_limit_bytes=67_043_328),
        )(x, meta, wg, wu, wd, sg, su, sd)
        return y.reshape(1, 1, T, D)

    tokens, experts, whole = P("dp", "ep", None, None), P("ep", None, None), P(None, None)
    return jax.shard_map(
        body, mesh=mesh,
        in_specs=(tokens, tokens, tokens, tokens, experts, experts, experts, whole, whole, whole),
        out_specs=tokens, check_vma=False)
```

time: 412 us -> 159 us (0.39)
  the two profiles are of different devices: /device:TPU:0 before, /device:TPU:1 now
where the time goes in v1:
time: 159 us; the launch traced here: 158 us
  Pallas kernels  154 us (97%)
  local copies, waits for them, and re-layouts  2.31 us (1%)
  other arithmetic  2.02 us (1%)
    pallas_call x1, Pallas kernels, body(): pl.pallas_call(kernel, name='moe', out_shape=(jax.ShapeDtypeStruct((T, D)...  154 us

profile of v1, /device:TPU:1, one launch (start us, length us, event | category | flops | bytes accessed | tf_op | source)
XLA Modules:
  0.0 158.4 jit_solution(4618069963065062813)
XLA Ops:
  0.0 0.7 fusion.2
  0.7 0.7 fusion.4
  1.4 0.6 maximum_bitcast_fusion.meta
  2.0 154.0 %moe.1 = (bf16[256,2048]{1,0:T(8,128)(2,1)}, bf16[2,8,256,2048]{3,2,1,0:T(8,128)(2,1)}) custom-call(bf16[256,2048]{1,0:T(8,128)(2,1)} %bitcast.11, f32[16,256]{1,0:T(8,128)} %maximum_bitcast_fusion.meta, bf16[4,2048,1408]{2,1,0:T(8,128)(2,1)} %wg.1, bf16[4,2048,1408]{2,1,0:T(8,128)(2,1)} %wu.1, bf16[4,1408,2048]{2,1,0:T(8,128)(2,1)} %wd.1, ...), custom_call_target="tpu_custom_call" | custom-call | tf_op jit(solution)/shard_map/moe/pallas_call | solution.py:382
  156.1 2.3 %copy.34 = bf16[1,1,256,2048]{3,2,1,0:T(8,128)(2,1)} copy(bf16[1,1,256,2048]{3,2,1,0:T(8,128)(2,1)} %bitcast.12) | data formatting | bytes 2097152
  (1 shorter events, 0.0 us)

commit v2 on v1

v2 whole, which is shorter than its diff:
```python
import functools

import jax
import jax.numpy as jnp
from jax import lax
from jax.experimental import pallas as pl
from jax.experimental.pallas import tpu as pltpu
from jax.sharding import PartitionSpec as P

MESH = pl.DeviceIdType.MESH
F32, BF16 = jnp.float32, jnp.bfloat16

T, D, F, TOP = 256, 2048, 1408, 6
SLOTS, PAD, EXP = 30, 32, 4
ROWS = EXP * PAD
HALF = D // 2
PART = ((0, 88), (88, 88), (176, 80))
BIT = (4, 2, 1)
ORDER = tuple(tuple((p + i) % 3 for i in range(3)) for p in range(3))


def gather_messages(p):
    b0, b1, b2 = (BIT[d] for d in ORDER[p])
    table = ((0, 0), (0, 1), (b0, 1), (0, 2), (b0, 2), (b1, 2), (b0 | b1, 2))
    return tuple((s, i, s ^ BIT[ORDER[p][i]]) for s, i in table)


def scatter_messages(p):
    b0, b1, b2 = (BIT[d] for d in ORDER[p])
    return (
        (b0 | b1 | b2, 0, ()), (b0 | b1, 0, ()), (b0 | b2, 0, ()), (b0, 0, ()),
        (b1 | b2, 1, (0,)), (b1, 1, (1,)), (b2, 2, (2, 4)),
    )


GATHER = tuple(gather_messages(p) for p in range(3))
SCATTER = tuple(scatter_messages(p) for p in range(3))
LAST = (3, 5, 6)
WA, WB, WT = 768, 512, 128


def kernel(x, expert, slot, gate, wg, wu, wd, sg, su, sd, y, xg, *scratch):
    (ga, ua, gb, ub, gu, d0, d1, z, extra, ob, dr, r0, r1, r2, s0, s1, s2, acc, xt, comb, h, mt,
     wsem, xsem, xs_s, xs_r, meta_s, meta_r, ag_s, ag_r, fw_s, fw_r, dr_s, dr_r, rs_s, rs_r) = scratch
    me = lax.axis_index("ep")
    c, q = me % 2, me // 2
    sib = me + 1 - 2 * c
    nbr = [me + (1 - 2 * ((me // (2 * b)) % 2)) * (2 * b) for b in BIT]
    mine = pl.ds(pl.multiple_of(c * HALF, HALF), HALF)
    theirs = pl.ds(pl.multiple_of((1 - c) * HALF, HALF), HALF)
    rbuf, sbuf = (r0, r1, r2), (s0, s1, s2)

    def remote(src, dst, send, recv, to):
        return pltpu.make_async_remote_copy(
            src_ref=src, dst_ref=dst, send_sem=send, recv_sem=recv, device_id={"ep": to}, device_id_type=MESH)

    def ag(k, p, m, first=False):
        s, i, land = GATHER[p][m]
        rows = pl.ds(*PART[p])
        src = x.at[rows, mine] if first else xg.at[k, s, rows, mine]
        return remote(src, xg.at[k, land, rows, mine], ag_s.at[k, p, m], ag_r.at[k, p, m], nbr[ORDER[p][i]])

    def fwd(k, p, m):
        rows = pl.ds(*PART[p])
        piece = xg.at[k, GATHER[p][m][2], rows, mine]
        return remote(piece, piece, fw_s.at[k, p, m], fw_r.at[k, p, m], sib)

    def fwd_in(k, p, m):
        rows = pl.ds(*PART[p])
        piece = xg.at[k, GATHER[p][m][2], rows, theirs]
        return remote(piece, piece, fw_s.at[k, p, m], fw_r.at[k, p, m], sib)

    def give(k, r):
        return remote(z.at[r // 2, :, pl.ds((r % 2) * HALF, HALF)], dr.at[k, r], dr_s.at[k, r], dr_r.at[k, r], sib)

    def give_own(half):
        src = extra if half else z.at[0, :, pl.ds(0, HALF)]
        return remote(src, dr.at[half, 0], dr_s.at[half, 0], dr_r.at[half, 0], sib)

    def rs(k, p, n):
        to = nbr[ORDER[p][SCATTER[p][n][1]]]
        if n in LAST:
            return remote(sbuf[p].at[n], rbuf[p].at[c, n], rs_s.at[k, p, n], rs_r.at[c, p, n], to - c + k)
        return remote(sbuf[p].at[n], rbuf[p].at[k, n], rs_s.at[k, p, n], rs_r.at[k, p, n], to)

    def rs_in(half, p, n):
        return remote(sbuf[p].at[n], rbuf[p].at[half, n], rs_s.at[half, p, n], rs_r.at[half, p, n], sib)

    def meta_copy(i):
        return remote(mt.at[0], mt.at[i], meta_s.at[i], meta_r.at[i], xor(me, i, 4))

    def xor(v, mask, bits):
        out = v
        for b in range(bits):
            if mask >> b & 1:
                out = out + (1 - 2 * ((v // (1 << b)) % 2)) * (1 << b)
        return out

    own_send = [remote(x.at[:, cols], xg.at[c, 0, :, cols], xs_s.at[n], xs_r.at[n], sib)
                for n, cols in enumerate((theirs, mine))]
    own_recv = [remote(x.at[:, cols], xg.at[1 - c, 0, :, cols], xs_s.at[n], xs_r.at[n], sib)
                for n, cols in enumerate((mine, theirs))]
    x_in = pltpu.make_async_copy(x, xt.at[0], xsem.at[0])

    def load_a(g, u):
        return [pltpu.make_async_copy(g(0, WA), ga, wsem.at[0]), pltpu.make_async_copy(u(0, WA), ua, wsem.at[1])]

    def load_b(g, u):
        return [
            pltpu.make_async_copy(g(WA, WB), gb, wsem.at[2]),
            pltpu.make_async_copy(u(WA, WB), ub, wsem.at[3]),
            pltpu.make_async_copy(g(WA + WB, WT), gu.at[:, pl.ds(0, WT)], wsem.at[4]),
            pltpu.make_async_copy(u(WA + WB, WT), gu.at[:, pl.ds(WT, WT)], wsem.at[5]),
        ]

    def load_d(d, n):
        return [pltpu.make_async_copy(d(n * HALF, HALF), (d0, d1)[n], wsem.at[6 + n])]

    def start(copies):
        for copy in copies:
            copy.start()

    def wait(copies):
        for copy in copies:
            copy.wait()

    def routed(ref, e):
        return lambda n, w: ref.at[e, :, pl.ds(n, w)]

    def shared_in(ref, i):
        return lambda n, w: ref.at[:, pl.ds(pl.multiple_of(i * F + n, 128), w)]

    def shared_out(i):
        return lambda n, w: sd.at[pl.ds(pl.multiple_of(i * F, 128), F), pl.ds(n, w)]

    def start_gather(k):
        @pl.when(c == k)
        def _():
            for m in (0, 1, 3):
                for p in range(3):
                    ag(k, p, m, first=True).start()

        @pl.when(c != k)
        def _():
            own_recv[0].wait_recv()
            for m in (0, 1, 3):
                for p in range(3):
                    ag(k, p, m).start()

    def arrive(k, m, sends):
        for p in range(3):
            ag(k, p, m).wait_recv()
            for n in sends:
                ag(k, p, n).start()
            fwd(k, p, m).start()

    def x_load(k, r, b):
        return pltpu.make_async_copy(xg.at[k, r], xt.at[b], xsem.at[b])

    def fetch(k, r, b):
        if r:
            landed(k, r)
            x_load(k, r, b).start()
            return

        @pl.when(c == k)
        def _():
            pltpu.make_async_copy(x, xt.at[b], xsem.at[b]).start()

        @pl.when(c != k)
        def _():
            own_recv[1].wait_recv()
            x_load(k, r, b).start()

    def landed(k, r):
        for p in range(3):
            for m in range(7):
                if GATHER[p][m][2] == r:
                    fwd_in(k, p, m).wait_recv()

    def dispatch(k, r, b):
        x_load(k, r, b).wait()
        table = mt[2 * r + (k + c) % 2]
        row = (lax.broadcasted_iota(jnp.int32, (ROWS, T), 0) + me * ROWS).astype(F32)
        pick = jnp.zeros((ROWS, T), F32)
        weight = jnp.zeros((ROWS, T), F32)
        for j in range(TOP):
            hit = table[j:j + 1, :] == row
            pick = jnp.where(hit, 1.0, pick)
            weight = jnp.where(hit, table[8 + j:9 + j, :], weight)
        comb[k, r] = weight.T
        for n in range(0, D, 512):
            rows = jnp.dot(pick.astype(BF16), xt[b, :, n:n + 512], preferred_element_type=F32).astype(BF16)
            for e in range(EXP):
                z[e, r * PAD:(r + 1) * PAD, n:n + 512] = rows[e * PAD:(e + 1) * PAD]

    def gated(g, u):
        return (g * (1.0 / (1.0 + jnp.exp(-g))) * u).astype(BF16)

    def dot(a, b):
        return jnp.dot(a, b, preferred_element_type=F32)

    def hidden_a(load):
        for n in range(0, WA, 256):
            h[:, n:n + 256] = gated(dot(load(), ga[:, n:n + 256]), dot(load(), ua[:, n:n + 256]))

    def hidden_b(load):
        for n in range(0, WB, 256):
            h[:, WA + n:WA + n + 256] = gated(dot(load(), gb[:, n:n + 256]), dot(load(), ub[:, n:n + 256]))
        both = dot(load(), gu[...])
        h[:, WA + WB:] = gated(both[:, :WT], both[:, WT:])

    def down(half, store):
        for n in range(0, HALF, 512):
            store(half * HALF + n, dot(h[...], (d0, d1)[half][:, n:n + 512]))

    def give_all(k):
        for r in (7, 6, 5, 3, 4, 2, 1):
            part = dot(comb[k, r].astype(BF16), ob[k, r, :, theirs])
            z[r // 2, :, (r % 2) * HALF:(r % 2) * HALF + HALF] = part.astype(BF16)
            give(k, r).start()

        @pl.when(c != k)
        def _():
            for half in range(2):
                part = dot(comb[k, 0].astype(BF16), ob[k, 0, :, half * HALF:half * HALF + HALF]).astype(BF16)
                if half:
                    extra[...] = part
                else:
                    z[0, :, :HALF] = part
                give_own(half).start()

    def gave_all(k):
        for r in range(1, 8):
            give(k, r).wait_send()

        @pl.when(c != k)
        def _():
            for half in range(2):
                give_own(half).wait_send()

    def term(k, p, r, cols, half):
        first, rows = PART[p]
        low = first // 16 * 16
        part = dot(comb[k, r, first:first + rows, :].astype(BF16), ob[k, r, :, cols])
        other = dr[half, r, low:first + rows, :].astype(F32)[first - low:]
        return part + other

    def send_sum(k, n):
        for p in range(3):
            r, _, joins = SCATTER[p][n]
            total = term(k, p, r, mine, k)
            for j in joins:
                rs(k, p, j).wait_recv()
                total = total + rbuf[p][k, j].astype(F32)
            if k == 1:
                rs(0, p, n).wait_send()
            sbuf[p][n] = total.astype(BF16)
            rs(k, p, n).start()

    def start_scatter(k):
        give(k, 7).wait_recv()
        send_sum(k, 0)
        for r in (6, 5, 3):
            give(k, r).wait_recv()
        send_sum(k, 1)
        send_sum(k, 2)
        for r in (4, 2, 1):
            give(k, r).wait_recv()
        send_sum(k, 3)

    def finish(k):
        @pl.when(c == k)
        def _():
            for half in range(2):
                give_own(half).wait_recv()
                cols = slice(half * HALF, half * HALF + HALF)
                for p in range(3):
                    first, rows = PART[p]
                    total = term(k, p, 0, cols, half)
                    for j in LAST:
                        rs_in(half, p, j).wait_recv()
                        total = total + rbuf[p][half, j].astype(F32)
                    y[first:first + rows, cols] = (acc[first:first + rows, cols] + total).astype(BF16)

    own_send[0].start()
    x_in.start()
    start(load_a(shared_in(sg, 0), shared_in(su, 0)))
    start(load_b(shared_in(sg, 0), shared_in(su, 0)))
    for n in range(2):
        start(load_d(shared_out(0), n))
    own_send[1].start()
    for j in range(TOP):
        row = jnp.where(slot[j] < SLOTS, expert[j] * PAD + slot[j], -1).astype(F32)
        mt[0, j:j + 1, :] = row
        mt[0, 8 + j:9 + j, :] = gate[j].astype(BF16).astype(F32)
    start_gather(0)
    acc[...] = jnp.zeros_like(acc)
    for i in range(1, 16):
        meta_copy(i).start()
    x_in.wait()

    @pl.loop(0, 2)
    def _(i):
        def following(ref, routed_ref, load):
            @pl.when(i == 0)
            def _():
                start(load(*(shared_in(v, 1) for v in ref)))

            @pl.when(i == 1)
            def _():
                start(load(*(routed(v, 0) for v in routed_ref)))

        wait(load_a(shared_in(sg, i), shared_in(su, i)))
        hidden_a(lambda: xt[0])
        following((sg, su), (wg, wu), load_a)
        wait(load_b(shared_in(sg, i), shared_in(su, i)))
        hidden_b(lambda: xt[0])
        following((sg, su), (wg, wu), load_b)

        def store(n, v):
            acc[:, n:n + 512] += v

        for half in range(2):
            wait(load_d(shared_out(i), half))
            down(half, store)

            @pl.when(i == 0)
            def _():
                start(load_d(shared_out(1), half))

            @pl.when(i == 1)
            def _():
                start(load_d(routed(wd, 0), half))

        @pl.when(i == 0)
        def _():
            arrive(0, 0, (2, 4))

    arrive(0, 1, (5,))
    for i in range(1, 16):
        meta_copy(i).wait_recv()
    ORDER_IN = (0, 4, 2, 1, 6, 5, 3, 7)
    AHEAD = 2

    def dispatch_all(k, waits):
        for n in range(8 + AHEAD):
            if n < 8:
                for m in waits.get(n, ()):
                    arrive(k, m, ())
                fetch(k, ORDER_IN[n], n % (AHEAD + 1))
            if n >= AHEAD:
                dispatch(k, ORDER_IN[n - AHEAD], (n - AHEAD) % (AHEAD + 1))

    arrive(0, 2, (6,))
    start_gather(1)
    arrive(0, 3, ())
    dispatch_all(0, {4: (4, 5), 7: (6,)})

    @pl.loop(0, 8)
    def _(i):
        k, e = i // 4, i % 4
        nxt = (i + 1) % 4
        wait(load_a(routed(wg, e), routed(wu, e)))
        hidden_a(lambda: z[e])

        @pl.when(i < 7)
        def _():
            start(load_a(routed(wg, nxt), routed(wu, nxt)))

        @pl.when(i == 7)
        def _():
            send_sum(0, 6)

        wait(load_b(routed(wg, e), routed(wu, e)))
        hidden_b(lambda: z[e])

        @pl.when(i < 7)
        def _():
            start(load_b(routed(wg, nxt), routed(wu, nxt)))

        @pl.when(i == 4)
        def _():
            send_sum(0, 4)

        @pl.when(i == 5)
        def _():
            send_sum(0, 5)

        def store(n, v):
            for r in range(8):
                ob[k, r, pl.ds(pl.multiple_of(e * PAD, PAD), PAD), n:n + 512] = v[r * PAD:(r + 1) * PAD].astype(BF16)

        for half in range(2):
            wait(load_d(routed(wd, e), half))
            down(half, store)

            @pl.when(i < 7)
            def _():
                start(load_d(routed(wd, nxt), half))

        @pl.when(i == 0)
        def _():
            arrive(1, 0, (2, 4))

        @pl.when(i == 1)
        def _():
            arrive(1, 1, (5,))

        @pl.when(i == 2)
        def _():
            arrive(1, 2, (6,))
            arrive(1, 3, ())

        @pl.when(i == 3)
        def _():
            give_all(0)
            start_scatter(0)
            gave_all(0)
            dispatch_all(1, {4: (4, 5), 7: (6,)})

    give_all(1)
    start_scatter(1)
    send_sum(1, 4)
    finish(0)
    send_sum(1, 5)
    send_sum(1, 6)
    finish(1)

    for copy in own_send:
        copy.wait_send()
    for i in range(1, 16):
        meta_copy(i).wait_send()
    for k in range(2):
        for p in range(3):
            for m in range(7):
                ag(k, p, m).wait_send()
                fwd(k, p, m).wait_send()
    gave_all(1)
    for p in range(3):
        for n in range(7):
            rs(1, p, n).wait_send()


def solution(mesh):
    dma = pltpu.SemaphoreType.DMA

    def body(x, expert, slot, gate, wg, wu, wd, sg, su, sd):
        x = x.reshape(T, D)
        expert, slot, gate = (v.transpose(0, 3, 1, 2).reshape(TOP, 1, T) for v in (expert, slot, gate))
        hbm, vmem = pl.BlockSpec(memory_space=pltpu.HBM), pl.BlockSpec(memory_space=pltpu.VMEM)
        y, _ = pl.pallas_call(
            kernel,
            name="moe",
            out_shape=(jax.ShapeDtypeStruct((T, D), BF16), jax.ShapeDtypeStruct((2, 8, T, D), BF16)),
            in_specs=[hbm, vmem, vmem, vmem, hbm, hbm, hbm, hbm, hbm, hbm],
            out_specs=(vmem, hbm),
            scratch_shapes=[
                *[pltpu.VMEM((D, n), BF16) for n in (WA, WA, WB, WB, 2 * WT)],
                *[pltpu.VMEM((F, HALF), BF16)] * 2,
                pltpu.VMEM((EXP, T, D), BF16),
                pltpu.VMEM((T, HALF), BF16),
                pltpu.VMEM((2, 8, ROWS, D), BF16),
                pltpu.VMEM((2, 8, T, HALF), BF16),
                *[pltpu.VMEM((2, 7, n, HALF), BF16) for _, n in PART],
                *[pltpu.VMEM((7, n, HALF), BF16) for _, n in PART],
                pltpu.VMEM((T, D), F32),
                pltpu.VMEM((3, T, D), BF16),
                pltpu.VMEM((2, 8, T, ROWS), F32),
                pltpu.VMEM((T, F), BF16),
                pltpu.VMEM((16, 16, T), F32),
                dma((8,)), dma((3,)), dma((2,)), dma((2,)), dma((16,)), dma((16,)),
                dma((2, 3, 7)), dma((2, 3, 7)), dma((2, 3, 7)), dma((2, 3, 7)),
                dma((2, 8)), dma((2, 8)), dma((2, 3, 7)), dma((2, 3, 7)),
            ],
            compiler_params=pltpu.CompilerParams(has_side_effects=True, vmem_limit_bytes=67_043_328),
        )(x, expert, slot, gate, wg, wu, wd, sg, su, sd)
        return y.reshape(1, 1, T, D)

    tokens, experts, whole = P("dp", "ep", None, None), P("ep", None, None), P(None, None)
    return jax.shard_map(
        body, mesh=mesh,
        in_specs=(tokens, tokens, tokens, tokens, experts, experts, experts, whole, whole, whole),
        out_specs=tokens, check_vma=False)
```

time: 159 us -> 143 us (0.90)
  Pallas kernels: 154 us -> 141 us
  other arithmetic: 2.02 us -> 0 us
    pallas_call x1, Pallas kernels: 154 us -> 141 us  [body(): pl.pallas_call(kernel, name='moe', out_shape=(jax.ShapeDtypeStruct((T, D)...]
where the time goes in v2:
time: 143 us
  Pallas kernels  141 us (99%)
  local copies, waits for them, and re-layouts  2.3 us (2%)
    pallas_call x1, Pallas kernels, body(): pl.pallas_call(kernel, name='moe', out_shape=(jax.ShapeDtypeStruct((T, D)...  141 us

profile of v2, /device:TPU:1, one launch (start us, length us, event | category | flops | bytes accessed | tf_op | source)
XLA Modules:
  0.0 143.1 jit_solution(4515328355482942175)
XLA Ops:
  0.0 140.8 %moe.1 = (bf16[256,2048]{1,0:T(8,128)(2,1)}, bf16[2,8,256,2048]{3,2,1,0:T(8,128)(2,1)}) custom-call(bf16[256,2048]{1,0:T(8,128)(2,1)} %bitcast.11, s32[6,1,256]{2,1,0:T(1,128)} %bitcast.13, s32[6,1,256]{2,1,0:T(1,128)} %bitcast.14, f32[6,1,256]{2,1,0:T(1,128)} %bitcast.15, bf16[4,2048,1408]{2,1,0:T(8,128)(2,1)} %wg.1, bf16[4,2048,1408]{2,1,0:T(8,128)(2,1)} %wu.1, ...), custom_call_target="tpu_custom_call" | custom-call | tf_op jit(solution)/shard_map/moe/pallas_call | solution.py:452
  140.8 2.3 %copy.12 = bf16[1,1,256,2048]{3,2,1,0:T(8,128)(2,1)} copy(bf16[1,1,256,2048]{3,2,1,0:T(8,128)(2,1)} %bitcast.12) | data formatting | bytes 2097152

commit v3 on v2

--- a/solution.py
+++ b/solution.py
@@ -40,8 +40,8 @@
 
 
 def kernel(x, expert, slot, gate, wg, wu, wd, sg, su, sd, y, xg, *scratch):
-    (ga, ua, gb, ub, gu, d0, d1, z, extra, ob, dr, r0, r1, r2, s0, s1, s2, acc, xt, comb, h, mt,
-     wsem, xsem, xs_s, xs_r, meta_s, meta_r, ag_s, ag_r, fw_s, fw_r, dr_s, dr_r, rs_s, rs_r) = scratch
+    (ga, ua, gb, ub, gu, d0, d1, z, ds, ob, dr, r0, r1, r2, s0, s1, s2, acc, xt, comb, h, mt, own, flat, ev, sv, gv,
+     wsem, xsem, ysem, tsem, xs_s, xs_r, meta_s, meta_r, ag_s, ag_r, fw_s, fw_r, dr_s, dr_r, rs_s, rs_r) = scratch
     me = lax.axis_index("ep")
     c, q = me % 2, me // 2
     sib = me + 1 - 2 * c
@@ -71,11 +71,10 @@
         return remote(piece, piece, fw_s.at[k, p, m], fw_r.at[k, p, m], sib)
 
     def give(k, r):
-        return remote(z.at[r // 2, :, pl.ds((r % 2) * HALF, HALF)], dr.at[k, r], dr_s.at[k, r], dr_r.at[k, r], sib)
+        return remote(ds.at[r], dr.at[k, r], dr_s.at[k, r], dr_r.at[k, r], sib)
 
     def give_own(half):
-        src = extra if half else z.at[0, :, pl.ds(0, HALF)]
-        return remote(src, dr.at[half, 0], dr_s.at[half, 0], dr_r.at[half, 0], sib)
+        return remote(ds.at[8 * half], dr.at[half, 0], dr_s.at[half, 0], dr_r.at[half, 0], sib)
 
     def rs(k, p, n):
         to = nbr[ORDER[p][SCATTER[p][n][1]]]
@@ -87,7 +86,7 @@
         return remote(sbuf[p].at[n], rbuf[p].at[half, n], rs_s.at[half, p, n], rs_r.at[half, p, n], sib)
 
     def meta_copy(i):
-        return remote(mt.at[0], mt.at[i], meta_s.at[i], meta_r.at[i], xor(me, i, 4))
+        return remote(own.at[i], mt.at[i], meta_s.at[i], meta_r.at[i], xor(me, i, 4))
 
     def xor(v, mask, bits):
         out = v
@@ -150,9 +149,12 @@
     def arrive(k, m, sends):
         for p in range(3):
             ag(k, p, m).wait_recv()
-            for n in sends:
+            for n in sends[:1]:
                 ag(k, p, n).start()
             fwd(k, p, m).start()
+        for p in range(3):
+            for n in sends[1:]:
+                ag(k, p, n).start()
 
     def x_load(k, r, b):
         return pltpu.make_async_copy(xg.at[k, r], xt.at[b], xsem.at[b])
@@ -180,8 +182,8 @@
 
     def dispatch(k, r, b):
         x_load(k, r, b).wait()
-        table = mt[2 * r + (k + c) % 2]
-        row = (lax.broadcasted_iota(jnp.int32, (ROWS, T), 0) + me * ROWS).astype(F32)
+        table = mt[2 * r + (k + c) % 2].astype(F32)
+        row = lax.broadcasted_iota(jnp.int32, (ROWS, T), 0).astype(F32)
         pick = jnp.zeros((ROWS, T), F32)
         weight = jnp.zeros((ROWS, T), F32)
         for j in range(TOP):
@@ -217,17 +219,14 @@
     def give_all(k):
         for r in (7, 6, 5, 3, 4, 2, 1):
             part = dot(comb[k, r].astype(BF16), ob[k, r, :, theirs])
-            z[r // 2, :, (r % 2) * HALF:(r % 2) * HALF + HALF] = part.astype(BF16)
+            ds[r] = part.astype(BF16)
             give(k, r).start()
 
         @pl.when(c != k)
         def _():
             for half in range(2):
-                part = dot(comb[k, 0].astype(BF16), ob[k, 0, :, half * HALF:half * HALF + HALF]).astype(BF16)
-                if half:
-                    extra[...] = part
-                else:
-                    z[0, :, :HALF] = part
+                part = dot(comb[k, 0].astype(BF16), ob[k, 0, :, half * HALF:half * HALF + HALF])
+                ds[8 * half] = part.astype(BF16)
                 give_own(half).start()
 
     def gave_all(k):
@@ -258,16 +257,11 @@
             sbuf[p][n] = total.astype(BF16)
             rs(k, p, n).start()
 
-    def start_scatter(k):
-        give(k, 7).wait_recv()
-        send_sum(k, 0)
-        for r in (6, 5, 3):
+    def scatter(k, rows, messages):
+        for r in rows:
             give(k, r).wait_recv()
-        send_sum(k, 1)
-        send_sum(k, 2)
-        for r in (4, 2, 1):
-            give(k, r).wait_recv()
-        send_sum(k, 3)
+        for n in messages:
+            send_sum(k, n)
 
     def finish(k):
         @pl.when(c == k)
@@ -281,20 +275,38 @@
                     for j in LAST:
                         rs_in(half, p, j).wait_recv()
                         total = total + rbuf[p][half, j].astype(F32)
-                    y[first:first + rows, cols] = (acc[first:first + rows, cols] + total).astype(BF16)
-
-    own_send[0].start()
+                    xt[0, first:first + rows, cols] = (acc[first:first + rows, cols] + total).astype(BF16)
+                result(half).start()
+
+    def result(half):
+        cols = pl.ds(half * HALF, HALF)
+        return pltpu.make_async_copy(xt.at[0, :, cols], y.at[:, cols], ysem.at[half])
+
+    tables = [pltpu.make_async_copy(a, b, tsem.at[n]) for n, (a, b) in enumerate(((expert, ev), (slot, sv), (gate, gv)))]
+    start(tables)
     x_in.start()
     start(load_a(shared_in(sg, 0), shared_in(su, 0)))
+    barrier = pltpu.get_barrier_semaphore()
+    for i in range(1, 16):
+        pl.semaphore_signal(barrier, inc=1, device_id={"ep": xor(me, i, 4)}, device_id_type=MESH)
+    pl.semaphore_wait(barrier, 15)
+    own_send[0].start()
+    own_send[1].start()
+    start_gather(0)
     start(load_b(shared_in(sg, 0), shared_in(su, 0)))
     for n in range(2):
         start(load_d(shared_out(0), n))
-    own_send[1].start()
+
+    wait(tables)
+    flat[...] = jnp.full_like(flat, -1)
     for j in range(TOP):
-        row = jnp.where(slot[j] < SLOTS, expert[j] * PAD + slot[j], -1).astype(F32)
-        mt[0, j:j + 1, :] = row
-        mt[0, 8 + j:9 + j, :] = gate[j].astype(BF16).astype(F32)
-    start_gather(0)
+        flat[j:j + 1, :] = jnp.where(sv[j] < SLOTS, ev[j] * PAD + sv[j], -1)
+    gates = jnp.concatenate([gv[j] for j in range(TOP)] + [jnp.zeros((2, T), F32)], axis=0)
+    for i in range(16):
+        row = flat[...] - xor(me, i, 4) * ROWS
+        row = jnp.where((row >= 0) & (row < ROWS), row, -1).astype(F32)
+        own[i] = jnp.concatenate([row, gates], axis=0).astype(BF16)
+    mt[0] = own[0]
     acc[...] = jnp.zeros_like(acc)
     for i in range(1, 16):
         meta_copy(i).start()
@@ -338,24 +350,30 @@
             arrive(0, 0, (2, 4))
 
     arrive(0, 1, (5,))
+    arrive(0, 3, ())
     for i in range(1, 16):
         meta_copy(i).wait_recv()
     ORDER_IN = (0, 4, 2, 1, 6, 5, 3, 7)
-    AHEAD = 2
-
-    def dispatch_all(k, waits):
-        for n in range(8 + AHEAD):
-            if n < 8:
-                for m in waits.get(n, ()):
-                    arrive(k, m, ())
-                fetch(k, ORDER_IN[n], n % (AHEAD + 1))
-            if n >= AHEAD:
-                dispatch(k, ORDER_IN[n - AHEAD], (n - AHEAD) % (AHEAD + 1))
-
+    BUFFERS = 3
+
+    def fetch_first(k):
+        for n in range(BUFFERS):
+            fetch(k, ORDER_IN[n], n)
+
+    def dispatch_all(k, events):
+        for n in range(8):
+            dispatch(k, ORDER_IN[n], n % BUFFERS)
+            for event in events.get(n, ()):
+                event()
+            if n + BUFFERS < 8:
+                fetch(k, ORDER_IN[n + BUFFERS], n % BUFFERS)
+
+    fetch(0, 0, 0)
+    fetch(0, 4, 1)
     arrive(0, 2, (6,))
     start_gather(1)
-    arrive(0, 3, ())
-    dispatch_all(0, {4: (4, 5), 7: (6,)})
+    fetch(0, 2, 2)
+    dispatch_all(0, {1: [lambda: arrive(0, 4, ()), lambda: arrive(0, 5, ())], 4: [lambda: arrive(0, 6, ())]})
 
     @pl.loop(0, 8)
     def _(i):
@@ -379,6 +397,10 @@
         def _():
             start(load_b(routed(wg, nxt), routed(wu, nxt)))
 
+        @pl.when(i == 3)
+        def _():
+            arrive(1, 4, ())
+
         @pl.when(i == 4)
         def _():
             send_sum(0, 4)
@@ -414,18 +436,29 @@
 
         @pl.when(i == 3)
         def _():
+            arrive(1, 5, ())
+            fetch_first(1)
             give_all(0)
-            start_scatter(0)
-            gave_all(0)
-            dispatch_all(1, {4: (4, 5), 7: (6,)})
-
+            arrive(1, 6, ())
+            scatter(0, (7,), (0,))
+            dispatch_all(1, {
+                3: [lambda: scatter(0, (6, 5, 3), (1, 2))],
+                6: [lambda: scatter(0, (4, 2, 1), (3,))],
+            })
+
+    gave_all(0)
     give_all(1)
-    start_scatter(1)
+    scatter(1, (7,), (0,))
+    scatter(1, (6, 5, 3), (1, 2))
+    scatter(1, (4, 2, 1), (3,))
     send_sum(1, 4)
     finish(0)
     send_sum(1, 5)
     send_sum(1, 6)
     finish(1)
+
+    for half in range(2):
+        result(half).wait()
 
     for copy in own_send:
         copy.wait_send()
@@ -448,18 +481,18 @@
     def body(x, expert, slot, gate, wg, wu, wd, sg, su, sd):
         x = x.reshape(T, D)
         expert, slot, gate = (v.transpose(0, 3, 1, 2).reshape(TOP, 1, T) for v in (expert, slot, gate))
-        hbm, vmem = pl.BlockSpec(memory_space=pltpu.HBM), pl.BlockSpec(memory_space=pltpu.VMEM)
+        hbm = pl.BlockSpec(memory_space=pltpu.HBM)
         y, _ = pl.pallas_call(
             kernel,
             name="moe",
             out_shape=(jax.ShapeDtypeStruct((T, D), BF16), jax.ShapeDtypeStruct((2, 8, T, D), BF16)),
-            in_specs=[hbm, vmem, vmem, vmem, hbm, hbm, hbm, hbm, hbm, hbm],
-            out_specs=(vmem, hbm),
+            in_specs=[hbm, hbm, hbm, hbm, hbm, hbm, hbm, hbm, hbm, hbm],
+            out_specs=(hbm, hbm),
             scratch_shapes=[
                 *[pltpu.VMEM((D, n), BF16) for n in (WA, WA, WB, WB, 2 * WT)],
                 *[pltpu.VMEM((F, HALF), BF16)] * 2,
                 pltpu.VMEM((EXP, T, D), BF16),
-                pltpu.VMEM((T, HALF), BF16),
+                pltpu.VMEM((9, T, HALF), BF16),
                 pltpu.VMEM((2, 8, ROWS, D), BF16),
                 pltpu.VMEM((2, 8, T, HALF), BF16),
                 *[pltpu.VMEM((2, 7, n, HALF), BF16) for _, n in PART],
@@ -468,12 +501,13 @@
                 pltpu.VMEM((3, T, D), BF16),
                 pltpu.VMEM((2, 8, T, ROWS), F32),
                 pltpu.VMEM((T, F), BF16),
-                pltpu.VMEM((16, 16, T), F32),
-                dma((8,)), dma((3,)), dma((2,)), dma((2,)), dma((16,)), dma((16,)),
+                pltpu.VMEM((16, 16, T), BF16), pltpu.VMEM((16, 16, T), BF16), pltpu.VMEM((8, T), jnp.int32),
+                pltpu.VMEM((TOP, 1, T), jnp.int32), pltpu.VMEM((TOP, 1, T), jnp.int32), pltpu.VMEM((TOP, 1, T), F32),
+                dma((8,)), dma((3,)), dma((2,)), dma((3,)), dma((2,)), dma((2,)), dma((16,)), dma((16,)),
                 dma((2, 3, 7)), dma((2, 3, 7)), dma((2, 3, 7)), dma((2, 3, 7)),
                 dma((2, 8)), dma((2, 8)), dma((2, 3, 7)), dma((2, 3, 7)),
             ],
-            compiler_params=pltpu.CompilerParams(has_side_effects=True, vmem_limit_bytes=67_043_328),
+            compiler_params=pltpu.CompilerParams(collective_id=0, has_side_effects=True, vmem_limit_bytes=67_043_328),
         )(x, expert, slot, gate, wg, wu, wd, sg, su, sd)
         return y.reshape(1, 1, T, D)
 

time: 143 us -> 134 us (0.937)
  Pallas kernels: 141 us -> 131 us
    pallas_call x1, Pallas kernels: 141 us -> 131 us  [body(): pl.pallas_call(kernel, name='moe', out_shape=(jax.ShapeDtypeStruct((T, D)...]
where the time goes in v3:
time: 134 us
  Pallas kernels  131 us (98%)
  local copies, waits for them, and re-layouts  2.3 us (2%)
    pallas_call x1, Pallas kernels, body(): pl.pallas_call(kernel, name='moe', out_shape=(jax.ShapeDtypeStruct((T, D)...  131 us

profile of v3, /device:TPU:1, one launch (start us, length us, event | category | flops | bytes accessed | tf_op | source)
XLA Modules:
  0.0 133.7 jit_solution(15224315340509571383)
XLA Ops:
  0.0 131.4 %moe.1 = (bf16[256,2048]{1,0:T(8,128)(2,1)}, bf16[2,8,256,2048]{3,2,1,0:T(8,128)(2,1)}) custom-call(bf16[256,2048]{1,0:T(8,128)(2,1)} %bitcast.11, s32[6,1,256]{2,1,0:T(1,128)} %bitcast.13, s32[6,1,256]{2,1,0:T(1,128)} %bitcast.14, f32[6,1,256]{2,1,0:T(1,128)} %bitcast.15, bf16[4,2048,1408]{2,1,0:T(8,128)(2,1)} %wg.1, bf16[4,2048,1408]{2,1,0:T(8,128)(2,1)} %wu.1, ...), custom_call_target="tpu_custom_call" | custom-call | tf_op jit(solution)/shard_map/moe/pallas_call | solution.py:485
  131.4 2.3 %copy.12 = bf16[1,1,256,2048]{3,2,1,0:T(8,128)(2,1)} copy(bf16[1,1,256,2048]{3,2,1,0:T(8,128)(2,1)} %bitcast.12) | data formatting | bytes 2097152

commit v4 on v3

v4 whole, which is shorter than its diff:
```python
import functools

import jax
import jax.numpy as jnp
from jax import lax
from jax.experimental import pallas as pl
from jax.experimental.pallas import tpu as pltpu
from jax.sharding import PartitionSpec as P

MESH = pl.DeviceIdType.MESH
F32, BF16 = jnp.float32, jnp.bfloat16

T, D, F, TOP = 256, 2048, 1408, 6
SLOTS, PAD, EXP = 30, 32, 4
ROWS = EXP * PAD
HALF = D // 2
PART = ((0, 88), (88, 88), (176, 80))
BIT = (4, 2, 1)
ORDER = tuple(tuple((p + i) % 3 for i in range(3)) for p in range(3))


def gather_messages(p):
    b0, b1, b2 = (BIT[d] for d in ORDER[p])
    table = ((0, 0), (0, 1), (b0, 1), (0, 2), (b0, 2), (b1, 2), (b0 | b1, 2))
    return tuple((s, i, s ^ BIT[ORDER[p][i]]) for s, i in table)


def scatter_messages(p):
    b0, b1, b2 = (BIT[d] for d in ORDER[p])
    return (
        (b0 | b1 | b2, 0, ()), (b0 | b1, 0, ()), (b0 | b2, 0, ()), (b0, 0, ()),
        (b1 | b2, 1, (0,)), (b1, 1, (1,)), (b2, 2, (2, 4)),
    )


GATHER = tuple(gather_messages(p) for p in range(3))
SCATTER = tuple(scatter_messages(p) for p in range(3))
GROUP = (None, 2, 2, 1, 2, 1, 1, 0)
LAST = (3, 5, 6)
PLACE = {0: 0, 1: 1, 2: 2, 4: 3}
WA, WB, WT = 768, 512, 128


def kernel(x, expert, slot, gate, wg, wu, wd, sg, su, sd, pt, rl, xg, *scratch):
    (ga, ua, gb, ub, gu, d0, d1, z, ds, ob, dr, r0, r1, r2, s0, s1, s2, acc, xt, comb, h, mt, own, flat, ev, sv, gv,
     wsem, xsem, psem, tsem, xs_s, xs_r, meta_s, meta_r, ag_s, ag_r, fw_s, fw_r, dr_s, dr_r, own_s, own_r, rs_s, rs_r) = scratch
    me = lax.axis_index("ep")
    c, q = me % 2, me // 2
    sib = me + 1 - 2 * c
    nbr = [me + (1 - 2 * ((me // (2 * b)) % 2)) * (2 * b) for b in BIT]
    mine = pl.ds(pl.multiple_of(c * HALF, HALF), HALF)
    theirs = pl.ds(pl.multiple_of((1 - c) * HALF, HALF), HALF)
    rbuf, sbuf = (r0, r1, r2), (s0, s1, s2)

    def remote(src, dst, send, recv, to):
        return pltpu.make_async_remote_copy(
            src_ref=src, dst_ref=dst, send_sem=send, recv_sem=recv, device_id={"ep": to}, device_id_type=MESH)

    def ag(k, p, m, first=False):
        s, i, land = GATHER[p][m]
        rows = pl.ds(*PART[p])
        src = x.at[rows, mine] if first else xg.at[k, s, rows, mine]
        return remote(src, xg.at[k, land, rows, mine], ag_s.at[k], ag_r.at[k, m], nbr[ORDER[p][i]])

    def ag_in(k, m):
        piece = xg.at[k, 0, :, mine]
        return remote(piece, piece, ag_s.at[k], ag_r.at[k, m], sib)

    def fwd(k, p, m):
        land = GATHER[p][m][2]
        piece = xg.at[k, land, pl.ds(*PART[p]), mine]
        return remote(piece, piece, fw_s.at[k], fw_r.at[k, land], sib)

    def fwd_in(k, r):
        piece = xg.at[k, r, :, theirs]
        return remote(piece, piece, fw_s.at[k], fw_r.at[k, r], sib)

    def gathered(k):
        sent = xg.at[k, pl.ds(0, 7), :, mine]
        return remote(sent, sent, ag_s.at[k], ag_r.at[k, 0], sib), remote(sent, sent, fw_s.at[k], fw_r.at[k, 0], sib)

    def give(k, r):
        return remote(ds.at[r], dr.at[k, r], dr_s.at[k], dr_r.at[k, GROUP[r]], sib)

    def give_in(k, n, g):
        return remote(ds.at[pl.ds(0, n)], dr.at[k, pl.ds(0, n)], dr_s.at[k], dr_r.at[k, g], sib)

    def give_own(half):
        return remote(ds.at[8 * half], dr.at[half, 0], own_s, own_r, sib)

    def gave_own():
        return remote(ds.at[pl.ds(0, 2)], dr.at[0, pl.ds(0, 2)], own_s, own_r, sib)

    def rs(k, p, n):
        to = nbr[ORDER[p][SCATTER[p][n][1]]]
        send = rs_s.at[k, n // 6]
        if n in LAST:
            return remote(sbuf[p].at[n], rl.at[LAST.index(n), pl.ds(*PART[p]), mine], send, rs_r.at[c, n], to - c + k)
        return remote(sbuf[p].at[n], rbuf[p].at[k, PLACE[n]], send, rs_r.at[k, n], to)

    def rs_in(k, n):
        piece = rl.at[0, :, mine]
        return remote(piece, piece, rs_s.at[k, 0], rs_r.at[k, n], sib)

    def rs_sent(k, g):
        sent = xg.at[k, pl.ds(0, 1 if g else 6), :, mine]
        return remote(sent, sent, rs_s.at[k, g], rs_r.at[k, 0], sib)

    def meta_copy(i):
        return remote(own.at[i], mt.at[i], meta_s, meta_r, xor(me, i, 4))

    def meta_all():
        return remote(own.at[pl.ds(1, 15)], mt.at[pl.ds(1, 15)], meta_s, meta_r, sib)

    def xor(v, mask, bits):
        out = v
        for b in range(bits):
            if mask >> b & 1:
                out = out + (1 - 2 * ((v // (1 << b)) % 2)) * (1 << b)
        return out

    own_send = [remote(x.at[:, cols], xg.at[c, 0, :, cols], xs_s.at[n], xs_r.at[n], sib)
                for n, cols in enumerate((theirs, mine))]
    own_recv = [remote(x.at[:, cols], xg.at[1 - c, 0, :, cols], xs_s.at[n], xs_r.at[n], sib)
                for n, cols in enumerate((mine, theirs))]
    x_in = pltpu.make_async_copy(x, xt.at[0], xsem.at[0])

    def load_a(g, u):
        return [pltpu.make_async_copy(g(0, WA), ga, wsem.at[0]), pltpu.make_async_copy(u(0, WA), ua, wsem.at[1])]

    def load_b(g, u):
        return [
            pltpu.make_async_copy(g(WA, WB), gb, wsem.at[2]),
            pltpu.make_async_copy(u(WA, WB), ub, wsem.at[3]),
            pltpu.make_async_copy(g(WA + WB, WT), gu.at[:, pl.ds(0, WT)], wsem.at[4]),
            pltpu.make_async_copy(u(WA + WB, WT), gu.at[:, pl.ds(WT, WT)], wsem.at[5]),
        ]

    def load_d(d):
        return [pltpu.make_async_copy(d(n * HALF, HALF), (d0, d1)[n], wsem.at[6 + n]) for n in range(2)]

    def start(copies):
        for copy in copies:
            copy.start()

    def wait(copies):
        for copy in copies:
            copy.wait()

    def routed(ref, e):
        return lambda n, w: ref.at[e, :, pl.ds(n, w)]

    def shared_in(ref, i):
        return lambda n, w: ref.at[:, pl.ds(pl.multiple_of(i * F + n, 128), w)]

    def shared_out(i):
        return lambda n, w: sd.at[pl.ds(pl.multiple_of(i * F, 128), F), pl.ds(n, w)]

    def start_gather(k):
        @pl.when(c == k)
        def _():
            for m in (0, 1, 3):
                for p in range(3):
                    ag(k, p, m, first=True).start()

        @pl.when(c != k)
        def _():
            own_recv[0].wait_recv()
            for m in (0, 1, 3):
                for p in range(3):
                    ag(k, p, m).start()

    def arrive(k, m, sends):
        ag_in(k, m).wait_recv()
        for n in sends:
            for p in range(3):
                ag(k, p, n).start()
        for p in range(3):
            fwd(k, p, m).start()

    def x_load(k, r, b):
        return pltpu.make_async_copy(xg.at[k, r], xt.at[b], xsem.at[b])

    def fetch(k, r, b):
        if r:
            fwd_in(k, r).wait_recv()
            x_load(k, r, b).start()
            return

        @pl.when(c == k)
        def _():
            pltpu.make_async_copy(x, xt.at[b], xsem.at[b]).start()

        @pl.when(c != k)
        def _():
            own_recv[1].wait_recv()
            x_load(k, r, b).start()

    def dispatch(k, r, b):
        x_load(k, r, b).wait()
        table = mt[2 * r + (k + c) % 2].astype(F32)
        row = lax.broadcasted_iota(jnp.int32, (ROWS, T), 0).astype(F32)
        pick = jnp.zeros((ROWS, T), F32)
        weight = jnp.zeros((ROWS, T), F32)
        for j in range(TOP):
            hit = table[j:j + 1, :] == row
            pick = jnp.where(hit, 1.0, pick)
            weight = jnp.where(hit, table[8 + j:9 + j, :], weight)
        comb[k, r] = weight.T
        for n in range(0, D, 512):
            rows = jnp.dot(pick.astype(BF16), xt[b, :, n:n + 512], preferred_element_type=F32).astype(BF16)
            for e in range(EXP):
                z[e, r * PAD:(r + 1) * PAD, n:n + 512] = rows[e * PAD:(e + 1) * PAD]

    def gated(g, u):
        return (g * (1.0 / (1.0 + jnp.exp(-g))) * u).astype(BF16)

    def dot(a, b):
        return jnp.dot(a, b, preferred_element_type=F32)

    def hidden_a(load):
        for n in range(0, WA, 256):
            h[:, n:n + 256] = gated(dot(load(), ga[:, n:n + 256]), dot(load(), ua[:, n:n + 256]))

    def hidden_b(load):
        for n in range(0, WB, 256):
            h[:, WA + n:WA + n + 256] = gated(dot(load(), gb[:, n:n + 256]), dot(load(), ub[:, n:n + 256]))
        both = dot(load(), gu[...])
        h[:, WA + WB:] = gated(both[:, :WT], both[:, WT:])

    def down(store):
        for half in range(2):
            for n in range(0, HALF, 512):
                store(half * HALF + n, dot(h[...], (d0, d1)[half][:, n:n + 512]))

    def give_some(k, rs):
        for r in rs:
            ds[r] = dot(comb[k, r].astype(BF16), ob[k, r, :, theirs]).astype(BF16)
            give(k, r).start()

    def give_owner(k):
        @pl.when(c != k)
        def _():
            for half in range(2):
                part = dot(comb[k, 0].astype(BF16), ob[k, 0, :, half * HALF:half * HALF + HALF])
                ds[8 * half] = part.astype(BF16)
                give_own(half).start()

    def gave_all(k):
        give_in(k, 7, 0).wait_send()

        @pl.when(c != k)
        def _():
            gave_own().wait_send()

    def term(k, p, r):
        first, rows = PART[p]
        low = first // 16 * 16
        part = dot(comb[k, r, first:first + rows, :].astype(BF16), ob[k, r, :, mine])
        other = dr[k, r, low:first + rows, :].astype(F32)[first - low:]
        return part + other

    def send_sum(k, n):
        for j in SCATTER[0][n][2]:
            rs_in(k, j).wait_recv()
        for p in range(3):
            r, _, joins = SCATTER[p][n]
            total = term(k, p, r)
            for j in joins:
                total = total + rbuf[p][k, PLACE[j]].astype(F32)
            sbuf[p][n] = total.astype(BF16)
            rs(k, p, n).start()

    def scatter(k, group, messages):
        give_in(k, 1 if group == 0 else 3, group).wait_recv()
        for n in messages:
            send_sum(k, n)

    def finish():
        gave_own().wait_recv()
        for half in range(2):
            cols = slice(half * HALF, half * HALF + HALF)
            acc[:, cols] += dot(comb[c, 0].astype(BF16), ob[c, 0, :, cols]) + dr[half, 0].astype(F32)
        result.start()

    result = pltpu.make_async_copy(acc, pt, psem)

    tables = [pltpu.make_async_copy(a, b, tsem.at[n]) for n, (a, b) in enumerate(((expert, ev), (slot, sv), (gate, gv)))]
    start(tables)
    x_in.start()
    start(load_a(shared_in(sg, 0), shared_in(su, 0)))
    barrier = pltpu.get_barrier_semaphore()
    for i in range(1, 16):
        pl.semaphore_signal(barrier, inc=1, device_id={"ep": xor(me, i, 4)}, device_id_type=MESH)
    pl.semaphore_wait(barrier, 15)
    own_send[0].start()
    own_send[1].start()
    start_gather(0)
    start(load_b(shared_in(sg, 0), shared_in(su, 0)))
    start(load_d(shared_out(0)))

    wait(tables)
    flat[...] = jnp.full_like(flat, -1)
    for j in range(TOP):
        flat[j:j + 1, :] = jnp.where(sv[j] < SLOTS, ev[j] * PAD + sv[j], -1)
    gates = jnp.concatenate([gv[j] for j in range(TOP)] + [jnp.zeros((2, T), F32)], axis=0)
    for i in range(16):
        row = flat[...] - xor(me, i, 4) * ROWS
        row = jnp.where((row >= 0) & (row < ROWS), row, -1).astype(F32)
        own[i] = jnp.concatenate([row, gates], axis=0).astype(BF16)
    mt[0] = own[0]
    acc[...] = jnp.zeros_like(acc)
    for i in range(1, 16):
        meta_copy(i).start()
    x_in.wait()

    @pl.loop(0, 2)
    def _(i):
        def following(ref, routed_ref, load):
            @pl.when(i == 0)
            def _():
                start(load(*(shared_in(v, 1) for v in ref)))

            @pl.when(i == 1)
            def _():
                start(load(*(routed(v, 0) for v in routed_ref)))

        wait(load_a(shared_in(sg, i), shared_in(su, i)))
        hidden_a(lambda: xt[0])
        following((sg, su), (wg, wu), load_a)
        wait(load_b(shared_in(sg, i), shared_in(su, i)))
        hidden_b(lambda: xt[0])
        following((sg, su), (wg, wu), load_b)

        def store(n, v):
            acc[:, n:n + 512] += v

        wait(load_d(shared_out(i)))
        down(store)

        @pl.when(i == 0)
        def _():
            start(load_d(shared_out(1)))

        @pl.when(i == 1)
        def _():
            start(load_d(routed(wd, 0)))

        @pl.when(i == 0)
        def _():
            arrive(0, 0, (2, 4))

    arrive(0, 1, (5,))
    arrive(0, 3, ())
    meta_all().wait_recv()
    ORDER_IN = (0, 4, 2, 1, 6, 5, 3, 7)
    BUFFERS = 3

    def run(k, steps):
        for step in steps:
            if callable(step):
                step()
            elif step > 0:
                fetch(k, ORDER_IN[step - 1], (step - 1) % BUFFERS)
            else:
                dispatch(k, ORDER_IN[-step - 1], (-step - 1) % BUFFERS)

    run(0, (1, 2, lambda: arrive(0, 2, (6,)), lambda: start_gather(1), 3, -1, 4, -2, lambda: arrive(0, 4, ()), -3, -4,
            lambda: arrive(0, 5, ()), 5, 6, 7, -5, -6, -7, lambda: arrive(0, 6, ()), 8, -8))

    @pl.loop(0, 8)
    def _(i):
        k, e = i // 4, i % 4
        nxt = (i + 1) % 4
        wait(load_a(routed(wg, e), routed(wu, e)))
        hidden_a(lambda: z[e])
        start(load_a(routed(wg, nxt), routed(wu, nxt)))
        wait(load_b(routed(wg, e), routed(wu, e)))
        hidden_b(lambda: z[e])
        start(load_b(routed(wg, nxt), routed(wu, nxt)))

        @pl.when(i == 0)
        def _():
            arrive(1, 0, (2, 4))

        @pl.when(i == 3)
        def _():
            arrive(1, 4, ())

        def store(n, v):
            for r in range(8):
                ob[k, r, pl.ds(pl.multiple_of(e * PAD, PAD), PAD), n:n + 512] = v[r * PAD:(r + 1) * PAD].astype(BF16)

        wait(load_d(routed(wd, e)))
        down(store)
        start(load_d(routed(wd, nxt)))

        @pl.when(i == 1)
        def _():
            arrive(1, 1, (5,))

        @pl.when(i == 2)
        def _():
            arrive(1, 2, (6,))
            arrive(1, 3, ())

        @pl.when(i == 3)
        def _():
            run(1, (
                1, 2, 3, lambda: arrive(1, 5, ()), lambda: give_some(0, (7, 6, 5, 3)), lambda: scatter(0, 0, (0,)),
                lambda: arrive(1, 6, ()), lambda: give_some(0, (4, 2, 1)), lambda: give_owner(0),
                -1, 4, -2, 5, -3, 6, -4, 7, lambda: scatter(0, 1, (1, 2)), -5, 8, -6, -7,
                lambda: scatter(0, 2, (3,)), -8))

        @pl.when(i == 4)
        def _():
            send_sum(0, 4)

        @pl.when(i == 5)
        def _():
            send_sum(0, 5)

        @pl.when(i == 6)
        def _():
            send_sum(0, 6)

    gave_all(0)
    give_some(1, (7, 6, 5, 3))
    rs_sent(0, 0).wait_send()
    scatter(1, 0, (0,))
    give_some(1, (4, 2, 1))
    scatter(1, 1, (1, 2))
    scatter(1, 2, (3,))
    give_owner(1)
    send_sum(1, 4)
    send_sum(1, 5)
    finish()
    wait(load_a(routed(wg, 0), routed(wu, 0)) + load_b(routed(wg, 0), routed(wu, 0)) + load_d(routed(wd, 0)))
    rs_sent(0, 1).wait_send()
    send_sum(1, 6)

    result.wait()
    for copy in own_send:
        copy.wait_send()
    meta_all().wait_send()
    for k in range(2):
        for copies in gathered(k):
            copies.wait_send()
    gave_all(1)
    for g in range(2):
        rs_sent(1, g).wait_send()
    for n in LAST:
        for half in range(2):
            rs_in(half, n).wait_recv()


def solution(mesh):
    dma = pltpu.SemaphoreType.DMA

    def body(x, expert, slot, gate, wg, wu, wd, sg, su, sd):
        x = x.reshape(T, D)
        expert, slot, gate = (v.transpose(0, 3, 1, 2).reshape(TOP, 1, T) for v in (expert, slot, gate))
        hbm = pl.BlockSpec(memory_space=pltpu.HBM)
        own, others, _ = pl.pallas_call(
            kernel,
            name="moe",
            out_shape=(
                jax.ShapeDtypeStruct((T, D), F32), jax.ShapeDtypeStruct((3, T, D), BF16),
                jax.ShapeDtypeStruct((2, 8, T, D), BF16)),
            in_specs=[hbm, hbm, hbm, hbm, hbm, hbm, hbm, hbm, hbm, hbm],
            out_specs=(hbm, hbm, hbm),
            scratch_shapes=[
                *[pltpu.VMEM((D, n), BF16) for n in (WA, WA, WB, WB, 2 * WT)],
                *[pltpu.VMEM((F, HALF), BF16)] * 2,
                pltpu.VMEM((EXP, T, D), BF16),
                pltpu.VMEM((9, T, HALF), BF16),
                pltpu.VMEM((2, 8, ROWS, D), BF16),
                pltpu.VMEM((2, 8, T, HALF), BF16),
                *[pltpu.VMEM((2, 4, n, HALF), BF16) for _, n in PART],
                *[pltpu.VMEM((7, n, HALF), BF16) for _, n in PART],
                pltpu.VMEM((T, D), F32),
                pltpu.VMEM((3, T, D), BF16),
                pltpu.VMEM((2, 8, T, ROWS), F32),
                pltpu.VMEM((T, F), BF16),
                pltpu.VMEM((16, 16, T), BF16), pltpu.VMEM((16, 16, T), BF16), pltpu.VMEM((8, T), jnp.int32),
                pltpu.VMEM((TOP, 1, T), jnp.int32), pltpu.VMEM((TOP, 1, T), jnp.int32), pltpu.VMEM((TOP, 1, T), F32),
                dma((8,)), dma((3,)), dma, dma((3,)), dma((2,)), dma((2,)), dma, dma,
                dma((2,)), dma((2, 7)), dma((2,)), dma((2, 8)), dma((2,)), dma((2, 3)), dma, dma,
                dma((2, 2)), dma((2, 7)),
            ],
            compiler_params=pltpu.CompilerParams(collective_id=0, has_side_effects=True, vmem_limit_bytes=67_043_328),
        )(x, expert, slot, gate, wg, wu, wd, sg, su, sd)
        for n in range(3):
            own = own + others[n].astype(F32)
        return own.astype(BF16).reshape(1, 1, T, D)

    tokens, experts, whole = P("dp", "ep", None, None), P("ep", None, None), P(None, None)
    return jax.shard_map(
        body, mesh=mesh,
        in_specs=(tokens, tokens, tokens, tokens, experts, experts, experts, whole, whole, whole),
        out_specs=tokens, check_vma=False)
```

time: 134 us -> 134 us (level)
  other arithmetic: 0 us -> 4.11 us
  local copies, waits for them, and re-layouts: 2.3 us -> 0 us
    reshape x0 -> x1, other arithmetic: none -> 4.11 us  [body(): return own.astype(BF16).reshape(1, 1, T, D)]
    unnamed x1 -> x0, local copies, waits for them, and re-layouts: 2.3 us -> none
    pallas_call x1, Pallas kernels: 131 us -> 130 us  [body(): pl.pallas_call(kernel, name='moe', out_shape=(jax.ShapeDtypeStruct((T, D)...]
where the time goes in v4:
time: 134 us
  Pallas kernels  130 us (97%)
  other arithmetic  4.11 us (3%)
    pallas_call x1, Pallas kernels, body(): pl.pallas_call(kernel, name='moe', out_shape=(jax.ShapeDtypeStruct((T, D)...  130 us
    reshape x1, other arithmetic, body(): return own.astype(BF16).reshape(1, 1, T, D)  4.11 us

profile of v4, /device:TPU:1, one launch (start us, length us, event | category | flops | bytes accessed | tf_op | source)
XLA Modules:
  0.0 134.1 jit_solution(5020718473078757970)
XLA Ops:
  0.0 130.0 %moe.1 = (f32[256,2048]{1,0:T(8,128)}, bf16[3,256,2048]{2,1,0:T(8,128)(2,1)}, bf16[2,8,256,2048]{3,2,1,0:T(8,128)(2,1)}) custom-call(bf16[256,2048]{1,0:T(8,128)(2,1)} %bitcast.21, s32[6,1,256]{2,1,0:T(1,128)} %bitcast.22, s32[6,1,256]{2,1,0:T(1,128)} %bitcast.23, f32[6,1,256]{2,1,0:T(1,128)} %bitcast.24, bf16[4,2048,1408]{2,1,0:T(8,128)(2,1)} %wg.1, ...), custom_call_target="tpu_custom_call" | custom-call | tf_op jit(solution)/shard_map/moe/pallas_call | solution.py:464
  130.0 4.1 %fusion.1 = bf16[1,1,256,2048]{3,2,1,0:T(8,128)(2,1)} fusion(f32[256,2048]{1,0:T(8,128)} %get-tuple-element.7, bf16[3,256,2048]{2,1,0:T(8,128)(2,1)} %get-tuple-element.8), kind=kLoop, calls=%fused_computation.4 | loop fusion | flops 3670016 | bytes 6291456 | tf_op jit(solution)/shard_map/reshape | solution.py:495

commit v5 on v4

--- a/solution.py
+++ b/solution.py
@@ -42,7 +42,7 @@
 
 
 def kernel(x, expert, slot, gate, wg, wu, wd, sg, su, sd, pt, rl, xg, *scratch):
-    (ga, ua, gb, ub, gu, d0, d1, z, ds, ob, dr, r0, r1, r2, s0, s1, s2, acc, xt, comb, h, mt, own, flat, ev, sv, gv,
+    (ga, ua, gb, ub, gu, d0, d1, z, ds, ob, dr, r0, r1, r2, l0, l1, l2, s0, s1, s2, acc, xt, comb, h, mt, own, flat, ev, sv, gv,
      wsem, xsem, psem, tsem, xs_s, xs_r, meta_s, meta_r, ag_s, ag_r, fw_s, fw_r, dr_s, dr_r, own_s, own_r, rs_s, rs_r) = scratch
     me = lax.axis_index("ep")
     c, q = me % 2, me // 2
@@ -50,7 +50,7 @@
     nbr = [me + (1 - 2 * ((me // (2 * b)) % 2)) * (2 * b) for b in BIT]
     mine = pl.ds(pl.multiple_of(c * HALF, HALF), HALF)
     theirs = pl.ds(pl.multiple_of((1 - c) * HALF, HALF), HALF)
-    rbuf, sbuf = (r0, r1, r2), (s0, s1, s2)
+    rbuf, lbuf, sbuf = (r0, r1, r2), (l0, l1, l2), (s0, s1, s2)
 
     def remote(src, dst, send, recv, to):
         return pltpu.make_async_remote_copy(
@@ -95,11 +95,12 @@
         to = nbr[ORDER[p][SCATTER[p][n][1]]]
         send = rs_s.at[k, n // 6]
         if n in LAST:
-            return remote(sbuf[p].at[n], rl.at[LAST.index(n), pl.ds(*PART[p]), mine], send, rs_r.at[c, n], to - c + k)
+            land = rl.at[pl.ds(*PART[p]), mine] if n == LAST[2] else lbuf[p].at[LAST.index(n), c]
+            return remote(sbuf[p].at[n], land, send, rs_r.at[c, n], to - c + k)
         return remote(sbuf[p].at[n], rbuf[p].at[k, PLACE[n]], send, rs_r.at[k, n], to)
 
     def rs_in(k, n):
-        piece = rl.at[0, :, mine]
+        piece = rl.at[:, mine]
         return remote(piece, piece, rs_s.at[k, 0], rs_r.at[k, n], sib)
 
     def rs_sent(k, g):
@@ -228,8 +229,8 @@
         both = dot(load(), gu[...])
         h[:, WA + WB:] = gated(both[:, :WT], both[:, WT:])
 
-    def down(store):
-        for half in range(2):
+    def down(store, halves=(0, 1)):
+        for half in halves:
             for n in range(0, HALF, 512):
                 store(half * HALF + n, dot(h[...], (d0, d1)[half][:, n:n + 512]))
 
@@ -281,6 +282,16 @@
         for half in range(2):
             cols = slice(half * HALF, half * HALF + HALF)
             acc[:, cols] += dot(comb[c, 0].astype(BF16), ob[c, 0, :, cols]) + dr[half, 0].astype(F32)
+
+    def finish_arrived():
+        for n in range(2):
+            for half in range(2):
+                rs_in(half, LAST[n]).wait_recv()
+        for half in range(2):
+            cols = slice(half * HALF, half * HALF + HALF)
+            for p in range(3):
+                first, rows = PART[p]
+                acc[first:first + rows, cols] += lbuf[p][0, half].astype(F32) + lbuf[p][1, half].astype(F32)
         result.start()
 
     result = pltpu.make_async_copy(acc, pt, psem)
@@ -374,10 +385,20 @@
         nxt = (i + 1) % 4
         wait(load_a(routed(wg, e), routed(wu, e)))
         hidden_a(lambda: z[e])
-        start(load_a(routed(wg, nxt), routed(wu, nxt)))
+        @pl.when(i < 7)
+        def _():
+            start(load_a(routed(wg, nxt), routed(wu, nxt)))
+
+        @pl.when(i == 7)
+        def _():
+            send_sum(0, 6)
+
         wait(load_b(routed(wg, e), routed(wu, e)))
         hidden_b(lambda: z[e])
-        start(load_b(routed(wg, nxt), routed(wu, nxt)))
+
+        @pl.when(i < 7)
+        def _():
+            start(load_b(routed(wg, nxt), routed(wu, nxt)))
 
         @pl.when(i == 0)
         def _():
@@ -386,14 +407,27 @@
         @pl.when(i == 3)
         def _():
             arrive(1, 4, ())
+            run(1, (1, 2, 3))
+
+        @pl.when(i == 4)
+        def _():
+            send_sum(0, 4)
+
+        @pl.when(i == 5)
+        def _():
+            send_sum(0, 5)
 
         def store(n, v):
             for r in range(8):
                 ob[k, r, pl.ds(pl.multiple_of(e * PAD, PAD), PAD), n:n + 512] = v[r * PAD:(r + 1) * PAD].astype(BF16)
 
-        wait(load_d(routed(wd, e)))
-        down(store)
-        start(load_d(routed(wd, nxt)))
+        for half in range(2):
+            wait(load_d(routed(wd, e))[half:half + 1])
+            down(store, (half,))
+
+            @pl.when(i < 7)
+            def _():
+                start(load_d(routed(wd, nxt))[half:half + 1])
 
         @pl.when(i == 1)
         def _():
@@ -407,22 +441,11 @@
         @pl.when(i == 3)
         def _():
             run(1, (
-                1, 2, 3, lambda: arrive(1, 5, ()), lambda: give_some(0, (7, 6, 5, 3)), lambda: scatter(0, 0, (0,)),
-                lambda: arrive(1, 6, ()), lambda: give_some(0, (4, 2, 1)), lambda: give_owner(0),
-                -1, 4, -2, 5, -3, 6, -4, 7, lambda: scatter(0, 1, (1, 2)), -5, 8, -6, -7,
+                lambda: arrive(1, 5, ()), lambda: give_some(0, (7, 6, 5, 3)), lambda: arrive(1, 6, ()),
+                -1, 4, -2, 5, lambda: scatter(0, 0, (0,)), lambda: give_some(0, (4, 2, 1)), lambda: give_owner(0),
+                -3, 6, -4, 7, lambda: scatter(0, 1, (1, 2)), -5, 8, -6, -7,
                 lambda: scatter(0, 2, (3,)), -8))
 
-        @pl.when(i == 4)
-        def _():
-            send_sum(0, 4)
-
-        @pl.when(i == 5)
-        def _():
-            send_sum(0, 5)
-
-        @pl.when(i == 6)
-        def _():
-            send_sum(0, 6)
 
     gave_all(0)
     give_some(1, (7, 6, 5, 3))
@@ -435,9 +458,9 @@
     send_sum(1, 4)
     send_sum(1, 5)
     finish()
-    wait(load_a(routed(wg, 0), routed(wu, 0)) + load_b(routed(wg, 0), routed(wu, 0)) + load_d(routed(wd, 0)))
     rs_sent(0, 1).wait_send()
     send_sum(1, 6)
+    finish_arrived()
 
     result.wait()
     for copy in own_send:
@@ -449,9 +472,8 @@
     gave_all(1)
     for g in range(2):
         rs_sent(1, g).wait_send()
-    for n in LAST:
-        for half in range(2):
-            rs_in(half, n).wait_recv()
+    for half in range(2):
+        rs_in(half, LAST[2]).wait_recv()
 
 
 def solution(mesh):
@@ -465,7 +487,7 @@
             kernel,
             name="moe",
             out_shape=(
-                jax.ShapeDtypeStruct((T, D), F32), jax.ShapeDtypeStruct((3, T, D), BF16),
+                jax.ShapeDtypeStruct((T, D), F32), jax.ShapeDtypeStruct((T, D), BF16),
                 jax.ShapeDtypeStruct((2, 8, T, D), BF16)),
             in_specs=[hbm, hbm, hbm, hbm, hbm, hbm, hbm, hbm, hbm, hbm],
             out_specs=(hbm, hbm, hbm),
@@ -477,6 +499,7 @@
                 pltpu.VMEM((2, 8, ROWS, D), BF16),
                 pltpu.VMEM((2, 8, T, HALF), BF16),
                 *[pltpu.VMEM((2, 4, n, HALF), BF16) for _, n in PART],
+                *[pltpu.VMEM((2, 2, n, HALF), BF16) for _, n in PART],
                 *[pltpu.VMEM((7, n, HALF), BF16) for _, n in PART],
                 pltpu.VMEM((T, D), F32),
                 pltpu.VMEM((3, T, D), BF16),
@@ -490,9 +513,7 @@
             ],
             compiler_params=pltpu.CompilerParams(collective_id=0, has_side_effects=True, vmem_limit_bytes=67_043_328),
         )(x, expert, slot, gate, wg, wu, wd, sg, su, sd)
-        for n in range(3):
-            own = own + others[n].astype(F32)
-        return own.astype(BF16).reshape(1, 1, T, D)
+        return (own + others.astype(F32)).astype(BF16).reshape(1, 1, T, D)
 
     tokens, experts, whole = P("dp", "ep", None, None), P("ep", None, None), P(None, None)
     return jax.shard_map(

time: 134 us -> 128 us (0.955)
  Pallas kernels: 130 us -> 125 us
    pallas_call x1, Pallas kernels: 130 us -> 125 us  [body(): pl.pallas_call(kernel, name='moe', out_shape=(jax.ShapeDtypeStruct((T, D)...]
where the time goes in v5:
time: 128 us
  Pallas kernels  125 us (98%)
  other arithmetic  3.11 us (2%)
    pallas_call x1, Pallas kernels, body(): pl.pallas_call(kernel, name='moe', out_shape=(jax.ShapeDtypeStruct((T, D)...  125 us
    reshape x1, other arithmetic, body(): return (own + others.astype(F32)).astype(BF16).reshape(1, 1, T, D)  3.11 us

profile of v5, /device:TPU:1, one launch (start us, length us, event | category | flops | bytes accessed | tf_op | source)
XLA Modules:
  0.0 127.8 jit_solution(8325049657883995430)
XLA Ops:
  0.0 124.7 %moe.1 = (f32[256,2048]{1,0:T(8,128)}, bf16[256,2048]{1,0:T(8,128)(2,1)}, bf16[2,8,256,2048]{3,2,1,0:T(8,128)(2,1)}) custom-call(bf16[256,2048]{1,0:T(8,128)(2,1)} %bitcast.12, s32[6,1,256]{2,1,0:T(1,128)} %bitcast.13, s32[6,1,256]{2,1,0:T(1,128)} %bitcast.14, f32[6,1,256]{2,1,0:T(1,128)} %bitcast.15, bf16[4,2048,1408]{2,1,0:T(8,128)(2,1)} %wg.1, ...), custom_call_target="tpu_custom_call" | custom-call | tf_op jit(solution)/shard_map/moe/pallas_call | solution.py:486
  124.7 3.1 %fusion = bf16[1,1,256,2048]{3,2,1,0:T(8,128)(2,1)} fusion(f32[256,2048]{1,0:T(8,128)} %get-tuple-element.7, bf16[256,2048]{1,0:T(8,128)(2,1)} %get-tuple-element.8), kind=kLoop, calls=%fused_computation.1 | loop fusion | flops 1572864 | bytes 4194304 | tf_op jit(solution)/shard_map/reshape | solution.py:516

commit v6 on v5

--- a/solution.py
+++ b/solution.py
@@ -448,10 +448,9 @@
 
 
     gave_all(0)
-    give_some(1, (7, 6, 5, 3))
+    give_some(1, (7, 6, 5, 3, 4, 2, 1))
     rs_sent(0, 0).wait_send()
     scatter(1, 0, (0,))
-    give_some(1, (4, 2, 1))
     scatter(1, 1, (1, 2))
     scatter(1, 2, (3,))
     give_owner(1)

time: 128 us -> 128 us (level)
  no operation moved by 1% of the time
where the time goes in v6:
time: 128 us
  Pallas kernels  125 us (98%)
  other arithmetic  3.11 us (2%)
    pallas_call x1, Pallas kernels, body(): pl.pallas_call(kernel, name='moe', out_shape=(jax.ShapeDtypeStruct((T, D)...  125 us
    reshape x1, other arithmetic, body(): return (own + others.astype(F32)).astype(BF16).reshape(1, 1, T, D)  3.11 us

profile of v6, /device:TPU:1, one launch (start us, length us, event | category | flops | bytes accessed | tf_op | source)
XLA Modules:
  0.0 127.8 jit_solution(7063157856010717398)
XLA Ops:
  0.0 124.7 %moe.1 = (f32[256,2048]{1,0:T(8,128)}, bf16[256,2048]{1,0:T(8,128)(2,1)}, bf16[2,8,256,2048]{3,2,1,0:T(8,128)(2,1)}) custom-call(bf16[256,2048]{1,0:T(8,128)(2,1)} %bitcast.12, s32[6,1,256]{2,1,0:T(1,128)} %bitcast.13, s32[6,1,256]{2,1,0:T(1,128)} %bitcast.14, f32[6,1,256]{2,1,0:T(1,128)} %bitcast.15, bf16[4,2048,1408]{2,1,0:T(8,128)(2,1)} %wg.1, ...), custom_call_target="tpu_custom_call" | custom-call | tf_op jit(solution)/shard_map/moe/pallas_call | solution.py:485
  124.7 3.1 %fusion = bf16[1,1,256,2048]{3,2,1,0:T(8,128)(2,1)} fusion(f32[256,2048]{1,0:T(8,128)} %get-tuple-element.7, bf16[256,2048]{1,0:T(8,128)(2,1)} %get-tuple-element.8), kind=kLoop, calls=%fused_computation.1 | loop fusion | flops 1572864 | bytes 4194304 | tf_op jit(solution)/shard_map/reshape | solution.py:515
